TPU v7x, 512 devices: a whole 4x8x8 slice. The times are simulated.
512 devices in a mesh: gx: 8 (over y), gy: 8 (over x, core), gz: 8 (over z).
Axes of the slice: x: 4, y: 8, z: 8, core: 2. Of those that a mesh axis runs over, the one named last changes fastest.
Arguments:
- pressure: float32 [96, 128, 1024], P('gx', 'gy', 'gz'), may hold values from -8 to 8
- wind: float32 [3, 96, 128, 1024], P(None, 'gx', 'gy', 'gz'), may hold values from -6 to 6
Outputs:
- result: float32 [96, 128, 1024], P('gx', 'gy', 'gz')
All inputs are finite; a program needn't handle non-finite values.
Results may differ from a plain program's by a relative error of at most 0.00019.
Values sent between devices are 32-bit elements; how exact they have to be, the bound alone decides.
A program may use at most 64 MiB of HBM per device.

v0:
```python
import jax
import jax.numpy as jnp
from jax import lax
from jax.sharding import PartitionSpec as P

SWEEPS = 2
COARSE_SWEEPS = 4


OMEGA = 0.8
VISCOSITY = 1.0
REACTION = 1.0


def extended(x, sides, width):
    edges = {}
    for axis, dim in sides:
        peers, length = (lax.axis_size(axis), x.shape[dim])
        up = [(i, (i + 1) % peers) for i in range(peers - 1)]
        last = lax.slice_in_dim(x, length - width, length, axis=dim)
        initial = lax.slice_in_dim(x, 0, width, axis=dim)
        edges[dim] = (
            lax.ppermute(last, axis, up),
            lax.ppermute(initial, axis, [(b, a) for a, b in up]),
        )
    done = []
    for _, dim in sides:
        low, high = edges[dim]
        around = [(width, width) if d in done else (0, 0) for d in range(x.ndim)]
        x = jnp.concatenate([jnp.pad(low, around), x, jnp.pad(high, around)], axis=dim)
        done.append(dim)
    return x


def with_halo(cells, sides, width):
    for axis, dim in sides:
        count = lax.axis_size(axis)
        ends = count - 1
        head = lax.slice_in_dim(cells, 0, width, axis=dim)
        tail = lax.slice_in_dim(cells, cells.shape[dim] - width, cells.shape[dim], axis=dim)
        cells = jnp.concatenate(
            [
                lax.ppermute(tail, axis, [(i, (i + 1) % count) for i in range(ends)]),
                cells,
                lax.ppermute(head, axis, [((i + 1) % count, i) for i in range(ends)]),
            ],
            axis=dim,
        )
    return cells


def six_sum(padded):
    return (
        padded[..., 2:, 1:-1, 1:-1]
        + padded[..., :-2, 1:-1, 1:-1]
        + padded[..., 1:-1, 2:, 1:-1]
        + padded[..., 1:-1, :-2, 1:-1]
        + padded[..., 1:-1, 1:-1, 2:]
        + padded[..., 1:-1, 1:-1, :-2]
    )


def central_parts(padded):
    return (
        (padded[..., 2:, 1:-1, 1:-1] - padded[..., :-2, 1:-1, 1:-1]) * 0.5,
        (padded[..., 1:-1, 2:, 1:-1] - padded[..., 1:-1, :-2, 1:-1]) * 0.5,
        (padded[..., 1:-1, 1:-1, 2:] - padded[..., 1:-1, 1:-1, :-2]) * 0.5,
    )


def crop(values, margin):
    return values[..., margin:-margin, margin:-margin, margin:-margin]


def axis_inside(position, extent, pieces, rim_width):
    places = position * extent + jnp.arange(-rim_width, extent + rim_width, dtype=jnp.int32)
    return ((places >= 0) & (places < extent * pieces)).astype(jnp.float32)


def inside_mask(extents, rim_width):
    along_x = axis_inside(lax.axis_index("gx"), extents[0], lax.axis_size("gx"), rim_width)
    along_y = axis_inside(lax.axis_index("gy"), extents[1], lax.axis_size("gy"), rim_width)
    along_z = axis_inside(lax.axis_index("gz"), extents[2], lax.axis_size("gz"), rim_width)
    return along_x[:, None, None] * along_y[None, :, None] * along_z[None, None, :]


def laplace(values, padded, weight_scale):
    return weight_scale * (6.0 * values - six_sum(padded))


def sweep(source, values, padded, weight_scale):
    return values + OMEGA / (6.0 * weight_scale) * (source - laplace(values, padded, weight_scale))


def start_sweep(source, weight_scale):
    return OMEGA / (6.0 * weight_scale) * source


def smooth_faces(values):
    return extended(values, (("gx", 0), ("gy", 1), ("gz", 2)), 1)


def smooth(source, values, weight_scale, sweep_count):
    for sweep_number in range(sweep_count):
        if values is None:
            values = start_sweep(source, weight_scale)
        else:
            values = sweep(source, values, smooth_faces(values), weight_scale)
    return values


def coarse_solve(source, weight_scale):
    reach = COARSE_SWEEPS - 1
    padded_source = with_halo(source, (("gx", 0), ("gy", 1), ("gz", 2)), reach)
    values = start_sweep(padded_source, weight_scale)
    for sweep_number in range(1, COARSE_SWEEPS):
        rim_width = reach - sweep_number
        values = sweep(crop(padded_source, sweep_number), crop(values, 1), values, weight_scale)
        if rim_width > 0:
            values = values * inside_mask(source.shape, rim_width)
    return values


def restrict(values):
    extent_x, extent_y, extent_z = values.shape
    blocks = values.reshape(extent_x // 2, 2, extent_y // 2, 2, extent_z // 2, 2)
    return 0.125 * jnp.sum(blocks, axis=(1, 3, 5))


def prolong(values):
    extent_x, extent_y, extent_z = values.shape
    spread = jnp.broadcast_to(
        values[:, None, :, None, :, None], (extent_x, 2, extent_y, 2, extent_z, 2)
    )
    return spread.reshape(2 * extent_x, 2 * extent_y, 2 * extent_z)


def vcycle(source, values, depth_index):
    weight_scale = 0.25**depth_index
    if depth_index == 2:
        return coarse_solve(source, weight_scale)
    values = smooth(source, values, weight_scale, SWEEPS)
    residual = source - laplace(values, smooth_faces(values), weight_scale)
    correction = vcycle(restrict(residual), None, depth_index + 1)
    values = values + prolong(correction)
    return smooth(source, values, weight_scale, SWEEPS)


def solve(source):
    values = None
    values = vcycle(source, values, 0)
    return values


def momentum(padded_velocity, wind):
    centre = padded_velocity[:, 1:-1, 1:-1, 1:-1]
    diffusion = 6.0 * centre - six_sum(padded_velocity)
    slopes = central_parts(padded_velocity)
    convection = wind[0:1] * slopes[0] + wind[1:2] * slopes[1] + wind[2:3] * slopes[2]
    return REACTION * centre + VISCOSITY * diffusion + convection


def body(pressure, wind):
    first = solve(pressure)
    padded_wind = with_halo(wind, (("gx", 1), ("gy", 2), ("gz", 3)), 1)
    padded = with_halo(first, (("gx", 0), ("gy", 1), ("gz", 2)), 3)
    velocity = jnp.stack(central_parts(padded)) * inside_mask(first.shape, 2)
    flux = momentum(velocity, padded_wind) * inside_mask(first.shape, 1)
    slopes = central_parts(flux)
    product = -(slopes[0][0] + slopes[1][1] + slopes[2][2])
    return solve(product)


def solution(mesh):
    in_specs = (P("gx", "gy", "gz"), P(None, "gx", "gy", "gz"))
    out_specs = P("gx", "gy", "gz")
    return jax.shard_map(body, mesh=mesh, in_specs=in_specs, out_specs=out_specs, check_vma=False)
```

profile of v0, /device:TPU:281, one launch (start us, length us, event | category | flops | bytes accessed | tf_op | source)
XLA Modules:
  0.0 483.9 jit_solution(412495087444313014)
XLA Ops:
  3.0 3.4 collective-permute-start.5
  16.1 4.4 collective-permute-start.1
  29.3 3.7 collective-permute-start.9
  34.9 5.0 %collective-permute-start.7 = (f32[1,16,128]{2,1,0:T(8,128)S(1)}, f32[1,16,128]{2,1,0:T(8,128)S(1)}, u32[]{:S(2)}, u32[]{:S(2)}) collective-permute-start(f32[1,16,128]{2,1,0:T(8,128)S(1)} %get-tuple-element.73), channel_id=1, source_target_pairs={{0,64},{64,128},{128,192},{192,256},{256,320},{320,384},{384,448},... | collective-permute-start | bytes 24584 | tf_op jit(solution)/shard_map/ppermute | solution.py:23
  40.9 7.7 %reshape.275 = f32[6,2,8,2,64,2]{5,4,3,2,1,0:T(8,128)} reshape(f32[12,16,128]{2,1,0:T(8,128)S(1)} %fusion.83) | data formatting | bytes 196608 | tf_op jit(solution)/shard_map/reshape | solution.py:126
  48.6 3.3 reduce_sum.36
  54.0 3.6 collective-permute-start.15
  59.6 4.8 collective-permute-start.13
  64.5 4.1 collective-permute-start.16
  70.5 3.4 collective-permute-start.60
  77.0 3.3 collective-permute-start.21
  82.2 4.6 collective-permute-start.19
  86.9 3.9 collective-permute-start.22
  106.0 4.7 collective-permute-start.26
  117.8 4.8 collective-permute-start.29
  127.1 3.6 collective-permute-start.33
  132.7 4.5 collective-permute-start.31
  137.3 4.9 %collective-permute-start.34 = (f32[6,8,1]{2,1,0:T(8,128)S(1)}, f32[6,8,1]{2,1,0:T(8,128)S(1)}, u32[]{:S(2)}, u32[]{:S(2)}) collective-permute-start(f32[6,8,1]{2,1,0:T(8,128)S(1)} %get-tuple-element.117), channel_id=1, source_target_pairs={{1,0},{2,1},{3,2},{4,3},{5,4},{6,5},{7,6},{9,8},{10,9},{11,10},{12... | collective-permute-start | bytes 584 | tf_op jit(solution)/shard_map/ppermute | solution.py:24
  144.2 4.3 collective-permute-done.35
  151.0 3.2 collective-permute-start.39
  156.2 4.6 collective-permute-start.37
  162.7 3.4 collective-permute-start.41
  169.0 3.5 broadcast_in_dim.9
  172.5 5.6 %reshape.278 = f32[12,16,128]{2,1,0:T(8,128)S(1)} reshape(f32[6,2,8,2,64,2]{5,4,3,2,1,0:T(8,128)} %broadcast_in_dim.9) | data formatting | bytes 196608 | tf_op jit(solution)/shard_map/reshape | solution.py:135
  182.7 3.4 collective-permute-start.47
  186.1 3.7 collective-permute-start.45
  191.8 4.6 collective-permute-start.43
  203.1 3.6 collective-permute-start.51
  214.1 4.6 collective-permute-start.49
  219.6 5.1 %collective-permute-start.54 = (f32[3,16,128]{2,1,0:T(8,128)S(1)}, f32[3,16,128]{2,1,0:T(8,128)S(1)}, u32[]{:S(2)}, u32[]{:S(2)}) collective-permute-start(f32[3,16,128]{2,1,0:T(8,128)S(1)} %get-tuple-element.57), channel_id=1, source_target_pairs={{0,64},{64,128},{128,192},{192,256},{256,320},{320,384},{384,448},... | collective-permute-start | bytes 73736 | tf_op jit(solution)/shard_map/ppermute | solution.py:43
  229.3 4.1 collective-permute-start.65
  233.4 4.9 %collective-permute-start.56 = (f32[18,3,128]{2,1,0:T(4,128)S(1)}, f32[18,3,128]{2,1,0:T(4,128)S(1)}, u32[]{:S(2)}, u32[]{:S(2)}) collective-permute-start(f32[18,3,128]{2,1,0:T(4,128)S(1)} %get-tuple-element.31), channel_id=1, source_target_pairs={{0,8},{8,16},{16,24},{24,32},{32,40},{40,48},{48,56},{1,9},{9,17},... | collective-permute-start | bytes 82952 | tf_op jit(solution)/shard_map/ppermute | solution.py:43
  246.4 5.1 %collective-permute-start.59 = (f32[18,22,3]{2,1,0:T(8,128)S(1)}, f32[18,22,3]{2,1,0:T(8,128)S(1)}, u32[]{:S(2)}, u32[]{:S(2)}) collective-permute-start(f32[18,22,3]{2,1,0:T(8,128)S(1)} %get-tuple-element.30), channel_id=1, source_target_pairs={{1,0},{2,1},{3,2},{4,3},{5,4},{6,5},{7,6},{9,8},{10,9},{11,10},{12... | collective-permute-start | bytes 14264 | tf_op jit(solution)/shard_map/ppermute | solution.py:45
  257.7 4.7 collective-permute-start.68
  267.1 4.6 collective-permute-start.67
  271.8 5.3 %collective-permute-start.70 = (f32[12,16,1]{2,1,0:T(8,128)S(1)}, f32[12,16,1]{2,1,0:T(8,128)S(1)}, u32[]{:S(2)}, u32[]{:S(2)}) collective-permute-start(f32[12,16,1]{2,1,0:T(8,128)S(1)} %get-tuple-element.51), channel_id=1, source_target_pairs={{1,0},{2,1},{3,2},{4,3},{5,4},{6,5},{7,6},{9,8},{10,9},{11,10},{12... | collective-permute-start | bytes 2312 | tf_op jit(solution)/shard_map/ppermute | solution.py:24
  279.1 5.1 %collective-permute-done.71 = f32[12,16,1]{2,1,0:T(8,128)S(1)} collective-permute-done((f32[12,16,1]{2,1,0:T(8,128)S(1)}, f32[12,16,1]{2,1,0:T(8,128)S(1)}, u32[]{:S(2)}, u32[]{:S(2)}) %collective-permute-start.71) | collective-permute-done | bytes 800 | tf_op jit(solution)/shard_map/ppermute | solution.py:23
  292.3 4.6 collective-permute-start.73
  298.9 3.4 collective-permute-start.77
  306.4 7.7 %reshape.279 = f32[6,2,8,2,64,2]{5,4,3,2,1,0:T(8,128)} reshape(f32[12,16,128]{2,1,0:T(8,128)S(1)} %fusion.34) | data formatting | bytes 196608 | tf_op jit(solution)/shard_map/reshape | solution.py:126
  314.1 3.3 reduce_sum.38
  324.9 4.6 collective-permute-start.79
  331.5 3.4 collective-permute-start.83
  337.5 3.4 collective-permute-start.86
  345.4 4.6 collective-permute-start.85
  352.0 3.4 collective-permute-start.89
  360.8 3.4 collective-permute-start.91
  366.4 5.3 %collective-permute-start.92 = (f32[9,3,32]{2,1,0:T(4,128)S(1)}, f32[9,3,32]{2,1,0:T(4,128)S(1)}, u32[]{:S(2)}, u32[]{:S(2)}) collective-permute-start(f32[9,3,32]{2,1,0:T(4,128)S(1)} %get-tuple-element.135), channel_id=1, source_target_pairs={{0,8},{8,16},{16,24},{24,32},{32,40},{40,48},{48,56},{1,9},{9,17},... | collective-permute-start | bytes 10376 | tf_op jit(solution)/shard_map/ppermute | solution.py:43
  379.3 4.1 collective-permute-start.95
  387.8 3.6 collective-permute-start.99
  393.9 4.1 collective-permute-start.97
  398.0 5.1 %collective-permute-start.100 = (f32[6,8,1]{2,1,0:T(8,128)S(1)}, f32[6,8,1]{2,1,0:T(8,128)S(1)}, u32[]{:S(2)}, u32[]{:S(2)}) collective-permute-start(f32[6,8,1]{2,1,0:T(8,128)S(1)} %get-tuple-element.93), channel_id=1, source_target_pairs={{1,0},{2,1},{3,2},{4,3},{5,4},{6,5},{7,6},{9,8},{10,9},{11,10},{12... | collective-permute-start | bytes 584 | tf_op jit(solution)/shard_map/ppermute | solution.py:24
  405.2 4.1 collective-permute-done.101
  411.7 3.7 collective-permute-start.105
  417.4 4.6 collective-permute-start.103
  423.9 3.6 collective-permute-start.107
  429.8 3.5 broadcast_in_dim.11
  433.4 5.6 %reshape.282 = f32[12,16,128]{2,1,0:T(8,128)S(1)} reshape(f32[6,2,8,2,64,2]{5,4,3,2,1,0:T(8,128)} %broadcast_in_dim.11) | data formatting | bytes 196608 | tf_op jit(solution)/shard_map/reshape | solution.py:135
  441.3 3.7 collective-permute-start.111
  447.0 4.6 collective-permute-start.109
  453.6 3.4 collective-permute-start.113
  463.5 3.3 collective-permute-start.117
  468.7 4.6 collective-permute-start.115
  475.3 3.4 collective-permute-start.119
  (354 shorter events, 208.7 us)
Async XLA Ops:
  1.1 19.5 %collective-permute-start.4 = (f32[12,16,1]{2,1,0:T(8,128)S(1)}, f32[12,16,1]{2,1,0:T(8,128)S(1)}, u32[]{:S(2)}, u32[]{:S(2)}) collective-permute-start(f32[12,16,1]{2,1,0:T(8,128)S(1)} %get-tuple-element.77), channel_id=1, source_target_pairs={{1,0},{2,1},{3,2},{4,3},{5,4},{6,5},{7,6},{9,8},{10,9},{11,10},{12... | collective-permute-start | bytes 2312 | tf_op jit(solution)/shard_map/ppermute | solution.py:24
  3.0 17.6 %collective-permute-start.5 = (f32[12,16,1]{2,1,0:T(8,128)S(1)}, f32[12,16,1]{2,1,0:T(8,128)S(1)}, u32[]{:S(2)}, u32[]{:S(2)}) collective-permute-start(f32[12,16,1]{2,1,0:T(8,128)S(1)} %get-tuple-element.78), channel_id=1, source_target_pairs={{0,1},{1,2},{2,3},{3,4},{4,5},{5,6},{6,7},{8,9},{9,10},{10,11},{11... | collective-permute-start | bytes 2312 | tf_op jit(solution)/shard_map/ppermute | solution.py:23
  21.5 13.4 %collective-permute-start.8 = (f32[12,1,128]{2,1,0:T(1,128)S(1)}, f32[12,1,128]{2,1,0:T(1,128)S(1)}, u32[]{:S(2)}, u32[]{:S(2)}) collective-permute-start(f32[12,1,128]{2,1,0:T(1,128)S(1)} %get-tuple-element.76), channel_id=1, source_target_pairs={{8,0},{16,8},{24,16},{32,24},{40,32},{48,40},{56,48},{9,1},{17,9},... | collective-permute-start | bytes 18440 | tf_op jit(solution)/shard_map/ppermute | solution.py:24
  24.0 16.0 %collective-permute-start.10 = (f32[12,16,1]{2,1,0:T(8,128)S(1)}, f32[12,16,1]{2,1,0:T(8,128)S(1)}, u32[]{:S(2)}, u32[]{:S(2)}) collective-permute-start(f32[12,16,1]{2,1,0:T(8,128)S(1)} %get-tuple-element.71), channel_id=1, source_target_pairs={{1,0},{2,1},{3,2},{4,3},{5,4},{6,5},{7,6},{9,8},{10,9},{11,10},{12... | collective-permute-start | bytes 2312 | tf_op jit(solution)/shard_map/ppermute | solution.py:24
  26.9 13.2 %collective-permute-start.11 = (f32[12,16,1]{2,1,0:T(8,128)S(1)}, f32[12,16,1]{2,1,0:T(8,128)S(1)}, u32[]{:S(2)}, u32[]{:S(2)}) collective-permute-start(f32[12,16,1]{2,1,0:T(8,128)S(1)} %get-tuple-element.72), channel_id=1, source_target_pairs={{0,1},{1,2},{2,3},{3,4},{4,5},{5,6},{6,7},{8,9},{9,10},{10,11},{11... | collective-permute-start | bytes 2312 | tf_op jit(solution)/shard_map/ppermute | solution.py:23
  51.9 16.6 %collective-permute-start.14 = (f32[6,1,64]{2,1,0:T(1,128)S(1)}, f32[6,1,64]{2,1,0:T(1,128)S(1)}, u32[]{:S(2)}, u32[]{:S(2)}) collective-permute-start(f32[6,1,64]{2,1,0:T(1,128)S(1)} %get-tuple-element.134), channel_id=1, source_target_pairs={{8,0},{16,8},{24,16},{32,24},{40,32},{48,40},{56,48},{9,1},{17,9},... | collective-permute-start | bytes 4616 | tf_op jit(solution)/shard_map/ppermute | solution.py:24
  54.0 16.5 %collective-permute-start.15 = (f32[6,1,64]{2,1,0:T(1,128)S(1)}, f32[6,1,64]{2,1,0:T(1,128)S(1)}, u32[]{:S(2)}, u32[]{:S(2)}) collective-permute-start(f32[6,1,64]{2,1,0:T(1,128)S(1)} %get-tuple-element.133), channel_id=1, source_target_pairs={{0,8},{8,16},{16,24},{24,32},{32,40},{40,48},{48,56},{1,9},{9,17},... | collective-permute-start | bytes 4616 | tf_op jit(solution)/shard_map/ppermute | solution.py:23
  57.6 16.9 %collective-permute-start.12 = (f32[1,8,64]{2,1,0:T(8,128)S(1)}, f32[1,8,64]{2,1,0:T(8,128)S(1)}, u32[]{:S(2)}, u32[]{:S(2)}) collective-permute-start(f32[1,8,64]{2,1,0:T(8,128)S(1)} %get-tuple-element.132), channel_id=1, source_target_pairs={{64,0},{128,64},{192,128},{256,192},{320,256},{384,320},{448,384},... | collective-permute-start | bytes 6152 | tf_op jit(solution)/shard_map/ppermute | solution.py:24
  59.6 15.0 %collective-permute-start.13 = (f32[1,8,64]{2,1,0:T(8,128)S(1)}, f32[1,8,64]{2,1,0:T(8,128)S(1)}, u32[]{:S(2)}, u32[]{:S(2)}) collective-permute-start(f32[1,8,64]{2,1,0:T(8,128)S(1)} %get-tuple-element.131), channel_id=1, source_target_pairs={{0,64},{64,128},{128,192},{192,256},{256,320},{320,384},{384,448},... | collective-permute-start | bytes 6152 | tf_op jit(solution)/shard_map/ppermute | solution.py:23
  70.5 42.1 %collective-permute-start.60 = (f32[3,1,16,128]{3,2,1,0:T(8,128)S(1)}, f32[3,1,16,128]{3,2,1,0:T(8,128)S(1)}, u32[]{:S(2)}, u32[]{:S(2)}) collective-permute-start(f32[3,1,16,128]{3,2,1,0:T(8,128)S(1)} %get-tuple-element.28), channel_id=1, source_target_pairs={{0,64},{64,128},{128,192},{192,256},{256,320},{320,384},{384,448},... | collective-permute-start | bytes 73736 | tf_op jit(solution)/shard_map/ppermute | solution.py:43
  74.7 12.2 %collective-permute-start.20 = (f32[6,1,64]{2,1,0:T(1,128)S(1)}, f32[6,1,64]{2,1,0:T(1,128)S(1)}, u32[]{:S(2)}, u32[]{:S(2)}) collective-permute-start(f32[6,1,64]{2,1,0:T(1,128)S(1)} %get-tuple-element.128), channel_id=1, source_target_pairs={{8,0},{16,8},{24,16},{32,24},{40,32},{48,40},{56,48},{9,1},{17,9},... | collective-permute-start | bytes 4616 | tf_op jit(solution)/shard_map/ppermute | solution.py:24
  77.0 13.8 %collective-permute-start.21 = (f32[6,1,64]{2,1,0:T(1,128)S(1)}, f32[6,1,64]{2,1,0:T(1,128)S(1)}, u32[]{:S(2)}, u32[]{:S(2)}) collective-permute-start(f32[6,1,64]{2,1,0:T(1,128)S(1)} %get-tuple-element.127), channel_id=1, source_target_pairs={{0,8},{8,16},{16,24},{24,32},{32,40},{40,48},{48,56},{1,9},{9,17},... | collective-permute-start | bytes 4616 | tf_op jit(solution)/shard_map/ppermute | solution.py:23
  80.3 16.7 %collective-permute-start.18 = (f32[1,8,64]{2,1,0:T(8,128)S(1)}, f32[1,8,64]{2,1,0:T(8,128)S(1)}, u32[]{:S(2)}, u32[]{:S(2)}) collective-permute-start(f32[1,8,64]{2,1,0:T(8,128)S(1)} %get-tuple-element.126), channel_id=1, source_target_pairs={{64,0},{128,64},{192,128},{256,192},{320,256},{384,320},{448,384},... | collective-permute-start | bytes 6152 | tf_op jit(solution)/shard_map/ppermute | solution.py:24
  82.2 14.7 %collective-permute-start.19 = (f32[1,8,64]{2,1,0:T(8,128)S(1)}, f32[1,8,64]{2,1,0:T(8,128)S(1)}, u32[]{:S(2)}, u32[]{:S(2)}) collective-permute-start(f32[1,8,64]{2,1,0:T(8,128)S(1)} %get-tuple-element.125), channel_id=1, source_target_pairs={{0,64},{64,128},{128,192},{192,256},{256,320},{320,384},{384,448},... | collective-permute-start | bytes 6152 | tf_op jit(solution)/shard_map/ppermute | solution.py:23
  92.8 29.8 %collective-permute-start.61 = (f32[3,1,16,128]{3,2,1,0:T(8,128)S(1)}, f32[3,1,16,128]{3,2,1,0:T(8,128)S(1)}, u32[]{:S(2)}, u32[]{:S(2)}) collective-permute-start(f32[3,1,16,128]{3,2,1,0:T(8,128)S(1)} %get-tuple-element.27), channel_id=1, source_target_pairs={{64,0},{128,64},{192,128},{256,192},{320,256},{384,320},{448,384},... | collective-permute-start | bytes 73736 | tf_op jit(solution)/shard_map/ppermute | solution.py:45
  125.1 17.1 %collective-permute-start.32 = (f32[6,1,64]{2,1,0:T(1,128)S(1)}, f32[6,1,64]{2,1,0:T(1,128)S(1)}, u32[]{:S(2)}, u32[]{:S(2)}) collective-permute-start(f32[6,1,64]{2,1,0:T(1,128)S(1)} %get-tuple-element.122), channel_id=1, source_target_pairs={{8,0},{16,8},{24,16},{32,24},{40,32},{48,40},{56,48},{9,1},{17,9},... | collective-permute-start | bytes 4616 | tf_op jit(solution)/shard_map/ppermute | solution.py:24
  127.1 17.1 %collective-permute-start.33 = (f32[6,1,64]{2,1,0:T(1,128)S(1)}, f32[6,1,64]{2,1,0:T(1,128)S(1)}, u32[]{:S(2)}, u32[]{:S(2)}) collective-permute-start(f32[6,1,64]{2,1,0:T(1,128)S(1)} %get-tuple-element.121), channel_id=1, source_target_pairs={{0,8},{8,16},{16,24},{24,32},{32,40},{40,48},{48,56},{1,9},{9,17},... | collective-permute-start | bytes 4616 | tf_op jit(solution)/shard_map/ppermute | solution.py:23
  130.7 17.8 %collective-permute-start.30 = (f32[1,8,64]{2,1,0:T(8,128)S(1)}, f32[1,8,64]{2,1,0:T(8,128)S(1)}, u32[]{:S(2)}, u32[]{:S(2)}) collective-permute-start(f32[1,8,64]{2,1,0:T(8,128)S(1)} %get-tuple-element.120), channel_id=1, source_target_pairs={{64,0},{128,64},{192,128},{256,192},{320,256},{384,320},{448,384},... | collective-permute-start | bytes 6152 | tf_op jit(solution)/shard_map/ppermute | solution.py:24
  132.7 15.8 %collective-permute-start.31 = (f32[1,8,64]{2,1,0:T(8,128)S(1)}, f32[1,8,64]{2,1,0:T(8,128)S(1)}, u32[]{:S(2)}, u32[]{:S(2)}) collective-permute-start(f32[1,8,64]{2,1,0:T(8,128)S(1)} %get-tuple-element.119), channel_id=1, source_target_pairs={{0,64},{64,128},{128,192},{192,256},{256,320},{320,384},{384,448},... | collective-permute-start | bytes 6152 | tf_op jit(solution)/shard_map/ppermute | solution.py:23
  148.6 14.1 %collective-permute-start.38 = (f32[6,1,64]{2,1,0:T(1,128)S(1)}, f32[6,1,64]{2,1,0:T(1,128)S(1)}, u32[]{:S(2)}, u32[]{:S(2)}) collective-permute-start(f32[6,1,64]{2,1,0:T(1,128)S(1)} %get-tuple-element.116), channel_id=1, source_target_pairs={{8,0},{16,8},{24,16},{32,24},{40,32},{48,40},{56,48},{9,1},{17,9},... | collective-permute-start | bytes 4616 | tf_op jit(solution)/shard_map/ppermute | solution.py:24
  151.0 15.1 %collective-permute-start.39 = (f32[6,1,64]{2,1,0:T(1,128)S(1)}, f32[6,1,64]{2,1,0:T(1,128)S(1)}, u32[]{:S(2)}, u32[]{:S(2)}) collective-permute-start(f32[6,1,64]{2,1,0:T(1,128)S(1)} %get-tuple-element.115), channel_id=1, source_target_pairs={{0,8},{8,16},{16,24},{24,32},{32,40},{40,48},{48,56},{1,9},{9,17},... | collective-permute-start | bytes 4616 | tf_op jit(solution)/shard_map/ppermute | solution.py:23
  154.2 14.6 %collective-permute-start.36 = (f32[1,8,64]{2,1,0:T(8,128)S(1)}, f32[1,8,64]{2,1,0:T(8,128)S(1)}, u32[]{:S(2)}, u32[]{:S(2)}) collective-permute-start(f32[1,8,64]{2,1,0:T(8,128)S(1)} %get-tuple-element.114), channel_id=1, source_target_pairs={{64,0},{128,64},{192,128},{256,192},{320,256},{384,320},{448,384},... | collective-permute-start | bytes 6152 | tf_op jit(solution)/shard_map/ppermute | solution.py:24
  156.2 12.7 %collective-permute-start.37 = (f32[1,8,64]{2,1,0:T(8,128)S(1)}, f32[1,8,64]{2,1,0:T(8,128)S(1)}, u32[]{:S(2)}, u32[]{:S(2)}) collective-permute-start(f32[1,8,64]{2,1,0:T(8,128)S(1)} %get-tuple-element.113), channel_id=1, source_target_pairs={{0,64},{64,128},{128,192},{192,256},{256,320},{320,384},{384,448},... | collective-permute-start | bytes 6152 | tf_op jit(solution)/shard_map/ppermute | solution.py:23
  178.2 13.5 %collective-permute-start.44 = (f32[12,1,128]{2,1,0:T(1,128)S(1)}, f32[12,1,128]{2,1,0:T(1,128)S(1)}, u32[]{:S(2)}, u32[]{:S(2)}) collective-permute-start(f32[12,1,128]{2,1,0:T(1,128)S(1)} %get-tuple-element.70), channel_id=1, source_target_pairs={{8,0},{16,8},{24,16},{32,24},{40,32},{48,40},{56,48},{9,1},{17,9},... | collective-permute-start | bytes 18440 | tf_op jit(solution)/shard_map/ppermute | solution.py:24
  180.8 18.1 %collective-permute-start.46 = (f32[12,16,1]{2,1,0:T(8,128)S(1)}, f32[12,16,1]{2,1,0:T(8,128)S(1)}, u32[]{:S(2)}, u32[]{:S(2)}) collective-permute-start(f32[12,16,1]{2,1,0:T(8,128)S(1)} %get-tuple-element.65), channel_id=1, source_target_pairs={{1,0},{2,1},{3,2},{4,3},{5,4},{6,5},{7,6},{9,8},{10,9},{11,10},{12... | collective-permute-start | bytes 2312 | tf_op jit(solution)/shard_map/ppermute | solution.py:24
  182.7 18.1 %collective-permute-start.47 = (f32[12,16,1]{2,1,0:T(8,128)S(1)}, f32[12,16,1]{2,1,0:T(8,128)S(1)}, u32[]{:S(2)}, u32[]{:S(2)}) collective-permute-start(f32[12,16,1]{2,1,0:T(8,128)S(1)} %get-tuple-element.66), channel_id=1, source_target_pairs={{0,1},{1,2},{2,3},{3,4},{4,5},{5,6},{6,7},{8,9},{9,10},{10,11},{11... | collective-permute-start | bytes 2312 | tf_op jit(solution)/shard_map/ppermute | solution.py:23
  196.4 17.6 %collective-permute-start.62 = (f32[3,14,1,128]{3,2,1,0:T(1,128)S(1)}, f32[3,14,1,128]{3,2,1,0:T(1,128)S(1)}, u32[]{:S(2)}, u32[]{:S(2)}) collective-permute-start(f32[3,14,1,128]{3,2,1,0:T(1,128)S(1)} %get-tuple-element.25), channel_id=1, source_target_pairs={{0,8},{8,16},{16,24},{24,32},{32,40},{40,48},{48,56},{1,9},{9,17},... | collective-permute-start | bytes 64520 | tf_op jit(solution)/shard_map/ppermute | solution.py:43
  198.9 19.7 %collective-permute-start.63 = (f32[3,14,1,128]{3,2,1,0:T(1,128)S(1)}, f32[3,14,1,128]{3,2,1,0:T(1,128)S(1)}, u32[]{:S(2)}, u32[]{:S(2)}) collective-permute-start(f32[3,14,1,128]{3,2,1,0:T(1,128)S(1)} %get-tuple-element.26), channel_id=1, source_target_pairs={{8,0},{16,8},{24,16},{32,24},{40,32},{48,40},{56,48},{9,1},{17,9},... | collective-permute-start | bytes 64520 | tf_op jit(solution)/shard_map/ppermute | solution.py:45
  206.8 12.0 %collective-permute-start.52 = (f32[12,16,1]{2,1,0:T(8,128)S(1)}, f32[12,16,1]{2,1,0:T(8,128)S(1)}, u32[]{:S(2)}, u32[]{:S(2)}) collective-permute-start(f32[12,16,1]{2,1,0:T(8,128)S(1)} %get-tuple-element.59), channel_id=1, source_target_pairs={{1,0},{2,1},{3,2},{4,3},{5,4},{6,5},{7,6},{9,8},{10,9},{11,10},{12... | collective-permute-start | bytes 2312 | tf_op jit(solution)/shard_map/ppermute | solution.py:24
  219.6 13.8 %collective-permute-start.54 = (f32[3,16,128]{2,1,0:T(8,128)S(1)}, f32[3,16,128]{2,1,0:T(8,128)S(1)}, u32[]{:S(2)}, u32[]{:S(2)}) collective-permute-start(f32[3,16,128]{2,1,0:T(8,128)S(1)} %get-tuple-element.57), channel_id=1, source_target_pairs={{0,64},{64,128},{128,192},{192,256},{256,320},{320,384},{384,448},... | collective-permute-start | bytes 73736 | tf_op jit(solution)/shard_map/ppermute | solution.py:43
  226.9 15.7 %collective-permute-start.64 = (f32[3,14,18,1]{3,2,1,0:T(8,128)S(1)}, f32[3,14,18,1]{3,2,1,0:T(8,128)S(1)}, u32[]{:S(2)}, u32[]{:S(2)}) collective-permute-start(f32[3,14,18,1]{3,2,1,0:T(8,128)S(1)} %get-tuple-element.20), channel_id=1, source_target_pairs={{0,1},{1,2},{2,3},{3,4},{4,5},{5,6},{6,7},{8,9},{9,10},{10,11},{11... | collective-permute-start | bytes 9080 | tf_op jit(solution)/shard_map/ppermute | solution.py:43
  229.3 14.2 %collective-permute-start.65 = (f32[3,14,18,1]{3,2,1,0:T(8,128)S(1)}, f32[3,14,18,1]{3,2,1,0:T(8,128)S(1)}, u32[]{:S(2)}, u32[]{:S(2)}) collective-permute-start(f32[3,14,18,1]{3,2,1,0:T(8,128)S(1)} %get-tuple-element.21), channel_id=1, source_target_pairs={{1,0},{2,1},{3,2},{4,3},{5,4},{6,5},{7,6},{9,8},{10,9},{11,10},{12... | collective-permute-start | bytes 9080 | tf_op jit(solution)/shard_map/ppermute | solution.py:45
  257.7 19.5 %collective-permute-start.68 = (f32[12,1,128]{2,1,0:T(1,128)S(1)}, f32[12,1,128]{2,1,0:T(1,128)S(1)}, u32[]{:S(2)}, u32[]{:S(2)}) collective-permute-start(f32[12,1,128]{2,1,0:T(1,128)S(1)} %get-tuple-element.56), channel_id=1, source_target_pairs={{8,0},{16,8},{24,16},{32,24},{40,32},{48,40},{56,48},{9,1},{17,9},... | collective-permute-start | bytes 18440 | tf_op jit(solution)/shard_map/ppermute | solution.py:24
  262.3 16.7 %collective-permute-start.69 = (f32[12,1,128]{2,1,0:T(1,128)S(1)}, f32[12,1,128]{2,1,0:T(1,128)S(1)}, u32[]{:S(2)}, u32[]{:S(2)}) collective-permute-start(f32[12,1,128]{2,1,0:T(1,128)S(1)} %get-tuple-element.55), channel_id=1, source_target_pairs={{0,8},{8,16},{16,24},{24,32},{32,40},{40,48},{48,56},{1,9},{9,17},... | collective-permute-start | bytes 18440 | tf_op jit(solution)/shard_map/ppermute | solution.py:23
  265.2 19.0 %collective-permute-start.66 = (f32[1,16,128]{2,1,0:T(8,128)S(1)}, f32[1,16,128]{2,1,0:T(8,128)S(1)}, u32[]{:S(2)}, u32[]{:S(2)}) collective-permute-start(f32[1,16,128]{2,1,0:T(8,128)S(1)} %get-tuple-element.54), channel_id=1, source_target_pairs={{64,0},{128,64},{192,128},{256,192},{320,256},{384,320},{448,384},... | collective-permute-start | bytes 24584 | tf_op jit(solution)/shard_map/ppermute | solution.py:24
  267.1 17.1 %collective-permute-start.67 = (f32[1,16,128]{2,1,0:T(8,128)S(1)}, f32[1,16,128]{2,1,0:T(8,128)S(1)}, u32[]{:S(2)}, u32[]{:S(2)}) collective-permute-start(f32[1,16,128]{2,1,0:T(8,128)S(1)} %get-tuple-element.53), channel_id=1, source_target_pairs={{0,64},{64,128},{128,192},{192,256},{256,320},{320,384},{384,448},... | collective-permute-start | bytes 24584 | tf_op jit(solution)/shard_map/ppermute | solution.py:23
  284.4 14.5 %collective-permute-start.74 = (f32[12,1,128]{2,1,0:T(1,128)S(1)}, f32[12,1,128]{2,1,0:T(1,128)S(1)}, u32[]{:S(2)}, u32[]{:S(2)}) collective-permute-start(f32[12,1,128]{2,1,0:T(1,128)S(1)} %get-tuple-element.50), channel_id=1, source_target_pairs={{8,0},{16,8},{24,16},{32,24},{40,32},{48,40},{56,48},{9,1},{17,9},... | collective-permute-start | bytes 18440 | tf_op jit(solution)/shard_map/ppermute | solution.py:24
  287.6 14.7 %collective-permute-start.75 = (f32[12,1,128]{2,1,0:T(1,128)S(1)}, f32[12,1,128]{2,1,0:T(1,128)S(1)}, u32[]{:S(2)}, u32[]{:S(2)}) collective-permute-start(f32[12,1,128]{2,1,0:T(1,128)S(1)} %get-tuple-element.49), channel_id=1, source_target_pairs={{0,8},{8,16},{16,24},{24,32},{32,40},{40,48},{48,56},{1,9},{9,17},... | collective-permute-start | bytes 18440 | tf_op jit(solution)/shard_map/ppermute | solution.py:23
  290.4 15.8 %collective-permute-start.72 = (f32[1,16,128]{2,1,0:T(8,128)S(1)}, f32[1,16,128]{2,1,0:T(8,128)S(1)}, u32[]{:S(2)}, u32[]{:S(2)}) collective-permute-start(f32[1,16,128]{2,1,0:T(8,128)S(1)} %get-tuple-element.48), channel_id=1, source_target_pairs={{64,0},{128,64},{192,128},{256,192},{320,256},{384,320},{448,384},... | collective-permute-start | bytes 24584 | tf_op jit(solution)/shard_map/ppermute | solution.py:24
  292.3 13.9 %collective-permute-start.73 = (f32[1,16,128]{2,1,0:T(8,128)S(1)}, f32[1,16,128]{2,1,0:T(8,128)S(1)}, u32[]{:S(2)}, u32[]{:S(2)}) collective-permute-start(f32[1,16,128]{2,1,0:T(8,128)S(1)} %get-tuple-element.47), channel_id=1, source_target_pairs={{0,64},{64,128},{128,192},{192,256},{256,320},{320,384},{384,448},... | collective-permute-start | bytes 24584 | tf_op jit(solution)/shard_map/ppermute | solution.py:23
  317.4 14.1 %collective-permute-start.80 = (f32[6,1,64]{2,1,0:T(1,128)S(1)}, f32[6,1,64]{2,1,0:T(1,128)S(1)}, u32[]{:S(2)}, u32[]{:S(2)}) collective-permute-start(f32[6,1,64]{2,1,0:T(1,128)S(1)} %get-tuple-element.110), channel_id=1, source_target_pairs={{8,0},{16,8},{24,16},{32,24},{40,32},{48,40},{56,48},{9,1},{17,9},... | collective-permute-start | bytes 4616 | tf_op jit(solution)/shard_map/ppermute | solution.py:24
  320.3 14.6 %collective-permute-start.81 = (f32[6,1,64]{2,1,0:T(1,128)S(1)}, f32[6,1,64]{2,1,0:T(1,128)S(1)}, u32[]{:S(2)}, u32[]{:S(2)}) collective-permute-start(f32[6,1,64]{2,1,0:T(1,128)S(1)} %get-tuple-element.109), channel_id=1, source_target_pairs={{0,8},{8,16},{16,24},{24,32},{32,40},{40,48},{48,56},{1,9},{9,17},... | collective-permute-start | bytes 4616 | tf_op jit(solution)/shard_map/ppermute | solution.py:23
  323.0 14.3 %collective-permute-start.78 = (f32[1,8,64]{2,1,0:T(8,128)S(1)}, f32[1,8,64]{2,1,0:T(8,128)S(1)}, u32[]{:S(2)}, u32[]{:S(2)}) collective-permute-start(f32[1,8,64]{2,1,0:T(8,128)S(1)} %get-tuple-element.108), channel_id=1, source_target_pairs={{64,0},{128,64},{192,128},{256,192},{320,256},{384,320},{448,384},... | collective-permute-start | bytes 6152 | tf_op jit(solution)/shard_map/ppermute | solution.py:24
  324.9 12.4 %collective-permute-start.79 = (f32[1,8,64]{2,1,0:T(8,128)S(1)}, f32[1,8,64]{2,1,0:T(8,128)S(1)}, u32[]{:S(2)}, u32[]{:S(2)}) collective-permute-start(f32[1,8,64]{2,1,0:T(8,128)S(1)} %get-tuple-element.107), channel_id=1, source_target_pairs={{0,64},{64,128},{128,192},{192,256},{256,320},{320,384},{384,448},... | collective-permute-start | bytes 6152 | tf_op jit(solution)/shard_map/ppermute | solution.py:23
  337.5 14.6 %collective-permute-start.86 = (f32[6,1,64]{2,1,0:T(1,128)S(1)}, f32[6,1,64]{2,1,0:T(1,128)S(1)}, u32[]{:S(2)}, u32[]{:S(2)}) collective-permute-start(f32[6,1,64]{2,1,0:T(1,128)S(1)} %get-tuple-element.104), channel_id=1, source_target_pairs={{8,0},{16,8},{24,16},{32,24},{40,32},{48,40},{56,48},{9,1},{17,9},... | collective-permute-start | bytes 4616 | tf_op jit(solution)/shard_map/ppermute | solution.py:24
  340.8 14.6 %collective-permute-start.87 = (f32[6,1,64]{2,1,0:T(1,128)S(1)}, f32[6,1,64]{2,1,0:T(1,128)S(1)}, u32[]{:S(2)}, u32[]{:S(2)}) collective-permute-start(f32[6,1,64]{2,1,0:T(1,128)S(1)} %get-tuple-element.103), channel_id=1, source_target_pairs={{0,8},{8,16},{16,24},{24,32},{32,40},{40,48},{48,56},{1,9},{9,17},... | collective-permute-start | bytes 4616 | tf_op jit(solution)/shard_map/ppermute | solution.py:23
  343.5 14.3 %collective-permute-start.84 = (f32[1,8,64]{2,1,0:T(8,128)S(1)}, f32[1,8,64]{2,1,0:T(8,128)S(1)}, u32[]{:S(2)}, u32[]{:S(2)}) collective-permute-start(f32[1,8,64]{2,1,0:T(8,128)S(1)} %get-tuple-element.102), channel_id=1, source_target_pairs={{64,0},{128,64},{192,128},{256,192},{320,256},{384,320},{448,384},... | collective-permute-start | bytes 6152 | tf_op jit(solution)/shard_map/ppermute | solution.py:24
  345.4 12.4 %collective-permute-start.85 = (f32[1,8,64]{2,1,0:T(8,128)S(1)}, f32[1,8,64]{2,1,0:T(8,128)S(1)}, u32[]{:S(2)}, u32[]{:S(2)}) collective-permute-start(f32[1,8,64]{2,1,0:T(8,128)S(1)} %get-tuple-element.101), channel_id=1, source_target_pairs={{0,64},{64,128},{128,192},{192,256},{256,320},{320,384},{384,448},... | collective-permute-start | bytes 6152 | tf_op jit(solution)/shard_map/ppermute | solution.py:23
  385.9 17.3 %collective-permute-start.98 = (f32[6,1,64]{2,1,0:T(1,128)S(1)}, f32[6,1,64]{2,1,0:T(1,128)S(1)}, u32[]{:S(2)}, u32[]{:S(2)}) collective-permute-start(f32[6,1,64]{2,1,0:T(1,128)S(1)} %get-tuple-element.98), channel_id=1, source_target_pairs={{8,0},{16,8},{24,16},{32,24},{40,32},{48,40},{56,48},{9,1},{17,9},... | collective-permute-start | bytes 4616 | tf_op jit(solution)/shard_map/ppermute | solution.py:24
  387.8 17.3 %collective-permute-start.99 = (f32[6,1,64]{2,1,0:T(1,128)S(1)}, f32[6,1,64]{2,1,0:T(1,128)S(1)}, u32[]{:S(2)}, u32[]{:S(2)}) collective-permute-start(f32[6,1,64]{2,1,0:T(1,128)S(1)} %get-tuple-element.97), channel_id=1, source_target_pairs={{0,8},{8,16},{16,24},{24,32},{32,40},{40,48},{48,56},{1,9},{9,17},... | collective-permute-start | bytes 4616 | tf_op jit(solution)/shard_map/ppermute | solution.py:23
  391.5 17.8 %collective-permute-start.96 = (f32[1,8,64]{2,1,0:T(8,128)S(1)}, f32[1,8,64]{2,1,0:T(8,128)S(1)}, u32[]{:S(2)}, u32[]{:S(2)}) collective-permute-start(f32[1,8,64]{2,1,0:T(8,128)S(1)} %get-tuple-element.96), channel_id=1, source_target_pairs={{64,0},{128,64},{192,128},{256,192},{320,256},{384,320},{448,384},... | collective-permute-start | bytes 6152 | tf_op jit(solution)/shard_map/ppermute | solution.py:24
  393.9 15.3 %collective-permute-start.97 = (f32[1,8,64]{2,1,0:T(8,128)S(1)}, f32[1,8,64]{2,1,0:T(8,128)S(1)}, u32[]{:S(2)}, u32[]{:S(2)}) collective-permute-start(f32[1,8,64]{2,1,0:T(8,128)S(1)} %get-tuple-element.95), channel_id=1, source_target_pairs={{0,64},{64,128},{128,192},{192,256},{256,320},{320,384},{384,448},... | collective-permute-start | bytes 6152 | tf_op jit(solution)/shard_map/ppermute | solution.py:23
  409.4 14.6 %collective-permute-start.104 = (f32[6,1,64]{2,1,0:T(1,128)S(1)}, f32[6,1,64]{2,1,0:T(1,128)S(1)}, u32[]{:S(2)}, u32[]{:S(2)}) collective-permute-start(f32[6,1,64]{2,1,0:T(1,128)S(1)} %get-tuple-element.92), channel_id=1, source_target_pairs={{8,0},{16,8},{24,16},{32,24},{40,32},{48,40},{56,48},{9,1},{17,9},... | collective-permute-start | bytes 4616 | tf_op jit(solution)/shard_map/ppermute | solution.py:24
  411.7 15.9 %collective-permute-start.105 = (f32[6,1,64]{2,1,0:T(1,128)S(1)}, f32[6,1,64]{2,1,0:T(1,128)S(1)}, u32[]{:S(2)}, u32[]{:S(2)}) collective-permute-start(f32[6,1,64]{2,1,0:T(1,128)S(1)} %get-tuple-element.91), channel_id=1, source_target_pairs={{0,8},{8,16},{16,24},{24,32},{32,40},{40,48},{48,56},{1,9},{9,17},... | collective-permute-start | bytes 4616 | tf_op jit(solution)/shard_map/ppermute | solution.py:23
  415.4 14.3 %collective-permute-start.102 = (f32[1,8,64]{2,1,0:T(8,128)S(1)}, f32[1,8,64]{2,1,0:T(8,128)S(1)}, u32[]{:S(2)}, u32[]{:S(2)}) collective-permute-start(f32[1,8,64]{2,1,0:T(8,128)S(1)} %get-tuple-element.90), channel_id=1, source_target_pairs={{64,0},{128,64},{192,128},{256,192},{320,256},{384,320},{448,384},... | collective-permute-start | bytes 6152 | tf_op jit(solution)/shard_map/ppermute | solution.py:24
  417.4 12.4 %collective-permute-start.103 = (f32[1,8,64]{2,1,0:T(8,128)S(1)}, f32[1,8,64]{2,1,0:T(8,128)S(1)}, u32[]{:S(2)}, u32[]{:S(2)}) collective-permute-start(f32[1,8,64]{2,1,0:T(8,128)S(1)} %get-tuple-element.89), channel_id=1, source_target_pairs={{0,64},{64,128},{128,192},{192,256},{256,320},{320,384},{384,448},... | collective-permute-start | bytes 6152 | tf_op jit(solution)/shard_map/ppermute | solution.py:23
  439.0 14.6 %collective-permute-start.110 = (f32[12,1,128]{2,1,0:T(1,128)S(1)}, f32[12,1,128]{2,1,0:T(1,128)S(1)}, u32[]{:S(2)}, u32[]{:S(2)}) collective-permute-start(f32[12,1,128]{2,1,0:T(1,128)S(1)} %get-tuple-element.44), channel_id=1, source_target_pairs={{8,0},{16,8},{24,16},{32,24},{40,32},{48,40},{56,48},{9,1},{17,9},... | collective-permute-start | bytes 18440 | tf_op jit(solution)/shard_map/ppermute | solution.py:24
  441.3 15.7 %collective-permute-start.111 = (f32[12,1,128]{2,1,0:T(1,128)S(1)}, f32[12,1,128]{2,1,0:T(1,128)S(1)}, u32[]{:S(2)}, u32[]{:S(2)}) collective-permute-start(f32[12,1,128]{2,1,0:T(1,128)S(1)} %get-tuple-element.43), channel_id=1, source_target_pairs={{0,8},{8,16},{16,24},{24,32},{32,40},{40,48},{48,56},{1,9},{9,17},... | collective-permute-start | bytes 18440 | tf_op jit(solution)/shard_map/ppermute | solution.py:23
  445.1 15.9 %collective-permute-start.108 = (f32[1,16,128]{2,1,0:T(8,128)S(1)}, f32[1,16,128]{2,1,0:T(8,128)S(1)}, u32[]{:S(2)}, u32[]{:S(2)}) collective-permute-start(f32[1,16,128]{2,1,0:T(8,128)S(1)} %get-tuple-element.42), channel_id=1, source_target_pairs={{64,0},{128,64},{192,128},{256,192},{320,256},{384,320},{448,384},... | collective-permute-start | bytes 24584 | tf_op jit(solution)/shard_map/ppermute | solution.py:24
  447.0 13.9 %collective-permute-start.109 = (f32[1,16,128]{2,1,0:T(8,128)S(1)}, f32[1,16,128]{2,1,0:T(8,128)S(1)}, u32[]{:S(2)}, u32[]{:S(2)}) collective-permute-start(f32[1,16,128]{2,1,0:T(8,128)S(1)} %get-tuple-element.41), channel_id=1, source_target_pairs={{0,64},{64,128},{128,192},{192,256},{256,320},{320,384},{384,448},... | collective-permute-start | bytes 24584 | tf_op jit(solution)/shard_map/ppermute | solution.py:23
  461.2 14.1 %collective-permute-start.116 = (f32[12,1,128]{2,1,0:T(1,128)S(1)}, f32[12,1,128]{2,1,0:T(1,128)S(1)}, u32[]{:S(2)}, u32[]{:S(2)}) collective-permute-start(f32[12,1,128]{2,1,0:T(1,128)S(1)} %get-tuple-element.38), channel_id=1, source_target_pairs={{8,0},{16,8},{24,16},{32,24},{40,32},{48,40},{56,48},{9,1},{17,9},... | collective-permute-start | bytes 18440 | tf_op jit(solution)/shard_map/ppermute | solution.py:24
  463.5 15.2 %collective-permute-start.117 = (f32[12,1,128]{2,1,0:T(1,128)S(1)}, f32[12,1,128]{2,1,0:T(1,128)S(1)}, u32[]{:S(2)}, u32[]{:S(2)}) collective-permute-start(f32[12,1,128]{2,1,0:T(1,128)S(1)} %get-tuple-element.37), channel_id=1, source_target_pairs={{0,8},{8,16},{16,24},{24,32},{32,40},{40,48},{48,56},{1,9},{9,17},... | collective-permute-start | bytes 18440 | tf_op jit(solution)/shard_map/ppermute | solution.py:23
  466.7 16.3 %collective-permute-start.114 = (f32[1,16,128]{2,1,0:T(8,128)S(1)}, f32[1,16,128]{2,1,0:T(8,128)S(1)}, u32[]{:S(2)}, u32[]{:S(2)}) collective-permute-start(f32[1,16,128]{2,1,0:T(8,128)S(1)} %get-tuple-element.36), channel_id=1, source_target_pairs={{64,0},{128,64},{192,128},{256,192},{320,256},{384,320},{448,384},... | collective-permute-start | bytes 24584 | tf_op jit(solution)/shard_map/ppermute | solution.py:24
  468.7 14.4 %collective-permute-start.115 = (f32[1,16,128]{2,1,0:T(8,128)S(1)}, f32[1,16,128]{2,1,0:T(8,128)S(1)}, u32[]{:S(2)}, u32[]{:S(2)}) collective-permute-start(f32[1,16,128]{2,1,0:T(8,128)S(1)} %get-tuple-element.35), channel_id=1, source_target_pairs={{0,64},{64,128},{128,192},{192,256},{256,320},{320,384},{384,448},... | collective-permute-start | bytes 24584 | tf_op jit(solution)/shard_map/ppermute | solution.py:23
  (58 other events, 475.7 us)
where the time goes:
time: 487 us; the launch traced here: 484 us
  starting transfers between devices  366 us (75%)
  waiting for transfers between devices  59.7 us (12%)
  local copies, waits for them, and re-layouts  39.9 us (8%)
  other arithmetic  16 us (3%)
    ppermute x48, starting transfers between devices, extended(): lax.ppermute(last, axis, up)  171 us
    ppermute x48, starting transfers between devices, extended(): lax.ppermute(initial, axis, [(b, a) for a, b in up])  120 us
    ppermute x12, starting transfers between devices, with_halo(): lax.ppermute(tail, axis, [(i, (i + 1) % count) for i in range(ends)])  39 us
    ppermute x48, waiting for transfers between devices, extended(): lax.ppermute(last, axis, up)  37.3 us
    ppermute x12, starting transfers between devices, with_halo(): lax.ppermute(head, axis, [((i + 1) % count, i) for i in range(ends)])  36 us
    reshape x4, local copies, waits for them, and re-layouts, restrict(): values.reshape(extent_x // 2, 2, extent_y // 2, 2, extent_z // 2, 2)  17 us
    ppermute x12, waiting for transfers between devices, with_halo(): lax.ppermute(head, axis, [((i + 1) % count, i) for i in range(ends)])  15.6 us
    reshape x4, local copies, waits for them, and re-layouts, prolong(): return spread.reshape(2 * extent_x, 2 * extent_y, 2 * extent_z)  12 us
  transfers between devices with their start and end apart: 120, of which 28 were waited for; matrix products, arithmetic and copies ran while one was open for 1% of the time, Pallas kernels for 0%

commit v1 on v0

v1 whole, which is shorter than its diff:
```python
import functools

import jax
import jax.numpy as jnp
from jax import lax
from jax.experimental import pallas as pl
from jax.experimental.pallas import tpu as pltpu
from jax.sharding import PartitionSpec as P

MESH = pl.DeviceIdType.MESH
AXES = ("gx", "gy", "gz")
BX, BY, BZ = 12, 16, 128
OMEGA = 0.8
KEEP = 1.0 - OMEGA
SIXTH = OMEGA / 6.0

AROUND = [
    (dx, dy, dz)
    for dz in (0, 1, -1)
    for dx in (0, 1, -1)
    for dy in (0, 1, -1)
    if (dx, dy, dz) != (0, 0, 0)
]
AROUND.sort(key=lambda d: -(abs(d[0]) + abs(d[1]) + abs(d[2])))
COARSE_X = [(2, 0, 0), (-2, 0, 0), (1, 0, 0), (-1, 0, 0)]
COARSE_YZ = [(0, dy, dz) for dz in (1, -1, 0) for dy in (2, -2, 1, -1, 0) if (dy, dz) != (0, 0)]
GREETED = AROUND + [d for d in COARSE_X + COARSE_YZ if d not in AROUND]


def part(delta, count, width):
    if delta == 0:
        return 0, 0, count
    if delta > 0:
        return count - width, -width, width
    return 0, count, width


class Place:
    def __init__(self, sizes):
        self.sizes = sizes
        self.at = [lax.axis_index(a) for a in AXES]
        self.has = []
        for g, n in zip(self.at, sizes):
            self.has.append({d: (g + d >= 0) & (g + d < n) for d in (-2, -1, 1, 2)})

    def exists(self, offset):
        found = None
        for table, d in zip(self.has, offset):
            if d:
                found = table[d] if found is None else found & table[d]
        return found

    def device(self, offset):
        return tuple(
            lax.rem(g + (d + n), n) if d else g for g, d, n in zip(self.at, offset, self.sizes)
        )


class Exchange:
    def __init__(self, place, copies, send_sems, recv_sems, base):
        self.place, self.items = place, []
        for k, (offset, src, dst) in enumerate(copies):
            copy = pltpu.make_async_remote_copy(
                src_ref=src,
                dst_ref=dst,
                send_sem=send_sems.at[base + k],
                recv_sem=recv_sems.at[base + k],
                device_id=place.device(offset),
                device_id_type=MESH,
            )
            self.items.append((offset, copy))

    def start(self):
        for offset, copy in self.items:
            pl.when(self.place.exists(offset))(copy.start)

    def wait_recv(self):
        for offset, copy in self.items:
            pl.when(self.place.exists(tuple(-d for d in offset)))(copy.wait_recv)

    def wait_send(self):
        for offset, copy in self.items:
            pl.when(self.place.exists(offset))(copy.wait_send)


def lanes(rows):
    return lax.broadcasted_iota(jnp.int32, (rows, 128), 1)


def row_mask(place, first_row, rows, extent):
    y = first_row + lax.broadcasted_iota(jnp.int32, (rows, 128), 0)
    low = jnp.where(place.has[1][-1], -64, 0)
    high = jnp.where(place.has[1][1], 64, extent)
    return (y >= low) & (y < high)


def rim_lanes(place, rows, start, right_end):
    lane = lanes(rows)
    right_stop = jnp.where(place.has[2][1], right_end, 0)
    left_start = jnp.where(place.has[2][-1], 120, 128)
    return ((lane >= start) & (lane < right_stop)) | (lane >= left_start)


def slab_weight(place, x, extent):
    if x < 0:
        return place.has[0][-1].astype(jnp.float32)
    if x >= extent:
        return place.has[0][1].astype(jnp.float32)
    return None


def z_back(a, h):
    lane0 = lanes(a.shape[0]) == 0
    ra, rh = pltpu.roll(a, 1, 1), pltpu.roll(h, 1, 1)
    return jnp.where(lane0, rh, ra), jnp.where(lane0, ra, rh)


def z_next(a, h):
    lane127 = lanes(a.shape[0]) == 127
    ra, rh = pltpu.roll(a, 127, 1), pltpu.roll(h, 127, 1)
    return jnp.where(lane127, rh, ra), jnp.where(lane127, ra, rh)


def masks0(place, first_row, rows):
    inner = row_mask(place, first_row, rows, BY)
    rim = inner & rim_lanes(place, rows, 0, 8)
    return inner.astype(jnp.float32), rim.astype(jnp.float32)


def scaled(value, mask, weight):
    value = value * mask
    return value if weight is None else value * weight


def six0(ref, i, r, n, rim=True):
    a, h = ref[0, i, r : r + n, :], ref[1, i, r : r + n, :]
    ba, bh = z_back(a, h)
    na, nh = z_next(a, h)
    out = []
    for t, (c, b, f) in enumerate(((a, ba, na), (h, bh, nh))):
        if t and not rim:
            break
        s = (
            (ref[t, i - 1, r : r + n, :] + ref[t, i + 1, r : r + n, :])
            + (ref[t, i, r - 1 : r - 1 + n, :] + ref[t, i, r + 1 : r + 1 + n, :])
            + (b + f)
        )
        out.append((c, s))
    return out


def six1(ref, i, r, n):
    c = ref[i, r : r + n, :]
    s = (
        (ref[i - 1, r : r + n, :] + ref[i + 1, r : r + n, :])
        + (ref[i, r - 1 : r - 1 + n, :] + ref[i, r + 1 : r + 1 + n, :])
        + (pltpu.roll(c, 1, 1) + pltpu.roll(c, 127, 1))
    )
    return c, s


def dot(a, b):
    return jnp.dot(
        a, b, precision=lax.Precision.HIGHEST, preferred_element_type=jnp.float32
    )


def pack0(load, store):
    lane = lanes(BY)
    first = jnp.zeros((BY, 128), jnp.float32)
    last = jnp.zeros((BY, 128), jnp.float32)
    for i in range(BX):
        turned = pltpu.roll(load(i), 8 * i, 1) if i else load(i)
        first = jnp.where((lane >= 8 * i) & (lane < 8 * i + 8), turned, first)
        at = (8 * i - 8) % 128
        last = jnp.where((lane >= at) & (lane < at + 8), turned, last)
    store(first, last)


def unpack0(land, x, rows):
    dx, i = (0, x) if 0 <= x < BX else ((-1, x + BX) if x < 0 else (1, x - BX))
    left, right = land[0, dx + 1], land[1, dx + 1]
    if i:
        left, right = pltpu.roll(left, 128 - 8 * i, 1), pltpu.roll(right, 128 - 8 * i, 1)
    lane = lanes(rows)
    return jnp.where(lane < 8, right, jnp.where(lane >= 120, left, 0.0))


def rim_copies(source, land):
    out = []
    for offset in AROUND:
        dx, dy, dz = offset
        if dz == 0:
            continue
        y0, yd, ny = part(dy, BY, 8)
        side = 0 if dz > 0 else 1
        out.append((offset, source(side, y0, ny), land(side, 1 - dx, yd, ny)))
    return out


def block_copies(source, land, h):
    out = []
    for offset in AROUND:
        dx, dy, dz = offset
        if dz != 0:
            continue
        x0, xd, nx = part(dx, BX, h)
        y0, yd, ny = part(dy, BY, 8)
        out.append((offset, source(x0, nx, y0, ny), land(xd, nx, yd, ny)))
    return out


def ordered(copies):
    return sorted(copies, key=lambda c: -sum(abs(d) for d in c[0]))


def kernel(
    sizes, p_ref, w_ref, out_ref,
    b0, v0, zs0, zr0, first, zsf, zrf, wind, zsw, zrw, velocity, flux,
    s1, l1, b1, v1, zs1, zr1, gathered, merged, c2, e2a, e2b,
    rows0, rows2, up1, up0, m_down0, m_down1, m_up1, m_up0,
    send_sems, recv_sems, load_sem,
):
    place = Place(sizes)

    load = pltpu.make_async_copy(w_ref, wind.at[:, 0, pl.ds(4, BX), pl.ds(8, BY), :], load_sem)
    for ref in (b0, zr0, first, zrf, zrw, l1, zr1, gathered):
        ref[...] = jnp.zeros(ref.shape, ref.dtype)
    wind[...] = jnp.zeros(wind.shape, wind.dtype)

    barrier = pltpu.get_barrier_semaphore()
    total = jnp.int32(0)
    for offset in GREETED:
        there = place.exists(offset)
        total = total + there.astype(jnp.int32)

        def greet(offset=offset):
            pl.semaphore_signal(
                barrier, inc=1, device_id=place.device(offset), device_id_type=MESH
            )

        pl.when(there)(greet)

    load.start()
    pack0(lambda i: p_ref[i], lambda f, l: (zs0.__setitem__(0, l), zs0.__setitem__(1, f)))
    for i in range(BX):
        b0[0, 3 + i, 8:24, :] = p_ref[i]
    for ref in (v0, velocity, flux, b1, v1, merged, c2, e2a, e2b, rows0, rows2, up1, up0):
        ref[...] = jnp.zeros(ref.shape, ref.dtype)

    k = lax.broadcasted_iota(jnp.int32, (128, 128), 0)
    l = lax.broadcasted_iota(jnp.int32, (128, 128), 1)
    m_down0[...] = (k // 2 == l).astype(jnp.float32) * 0.125
    for i in range(3):
        m_down1[i * 128 : i * 128 + 128, :] = (
            (l // 32 == i) & (k // 2 == l % 32)
        ).astype(jnp.float32) * 0.125
    m_up1[...] = (((l < 72) & (k == l // 2)) | ((l >= 120) & (k == 64 + l // 2))).astype(jnp.float32)
    m_up0[:, 0:128] = (k == l // 2).astype(jnp.float32)
    m_up0[:, 128:256] = (((l < 8) | (l >= 120)) & (k == 64 + l // 2)).astype(jnp.float32)

    def rows8(ref, x, nx, y, ny, lead):
        return ref.at[pl.ds(x, nx), pl.ds(y + lead, ny), :]

    ex0 = Exchange(place, ordered(
        block_copies(
            lambda x, nx, y, ny: p_ref.at[pl.ds(x, nx), pl.ds(y, ny), :],
            lambda x, nx, y, ny: b0.at[0, pl.ds(x + 3, nx), pl.ds(y + 8, ny), :], 3)
        + rim_copies(
            lambda s, y, ny: zs0.at[s, pl.ds(y, ny), :],
            lambda s, dx, y, ny: zr0.at[s, dx, pl.ds(y + 8, ny), :])
    ), send_sems, recv_sems, 0)
    exw = Exchange(place, ordered(
        block_copies(
            lambda x, nx, y, ny: w_ref.at[:, pl.ds(x, nx), pl.ds(y, ny), :],
            lambda x, nx, y, ny: wind.at[:, 0, pl.ds(x + 4, nx), pl.ds(y + 8, ny), :], 4)
        + rim_copies(
            lambda s, y, ny: zsw.at[s, :, pl.ds(y, ny), :],
            lambda s, dx, y, ny: zrw.at[s, dx, :, pl.ds(y + 8, ny), :])
    ), send_sems, recv_sems, 26)
    exf = Exchange(place, ordered(
        block_copies(
            lambda x, nx, y, ny: first.at[0, pl.ds(x + 6, nx), pl.ds(y + 16, ny), :],
            lambda x, nx, y, ny: first.at[0, pl.ds(x + 6, nx), pl.ds(y + 16, ny), :], 6)
        + rim_copies(
            lambda s, y, ny: zsf.at[s, pl.ds(y, ny), :],
            lambda s, dx, y, ny: zrf.at[s, dx, pl.ds(y + 8, ny), :])
    ), send_sems, recv_sems, 52)

    def level1_exchange(solve, base):
        out = []
        for offset in AROUND:
            dx, dy, dz = offset
            if dz == 0:
                x0, xd, nx = part(dx, 6, 4)
                out.append((
                    offset,
                    s1.at[solve, pl.ds(x0, nx)],
                    l1.at[solve, pl.ds(xd + 4, nx), pl.ds(8 - 8 * dy, 8), :],
                ))
            else:
                side = 0 if dz > 0 else 1
                out.append((
                    offset, zs1.at[solve, side], zr1.at[solve, side, 1 - dx, pl.ds(8 - 8 * dy, 8), :],
                ))
        return Exchange(place, ordered(out), send_sems, recv_sems, base)

    def coarse_exchanges(solve, base):
        a = [(d, gathered.at[solve, 2, 1, 2], gathered.at[solve, 2, 1, 2 - d[0]]) for d in COARSE_X]
        b = [(d, gathered.at[solve, 2, 1], gathered.at[solve, 2 - d[1], 1 - d[2]]) for d in COARSE_YZ]
        return (
            Exchange(place, a, send_sems, recv_sems, base),
            Exchange(place, b, send_sems, recv_sems, base + 4),
        )

    pl.semaphore_wait(barrier, total)
    ex0.start()

    load.wait()

    def store_wind_pack(d):
        def store(f, l):
            zsw[0, d] = l
            zsw[1, d] = f
        return store

    for d in range(3):
        pack0(lambda i: wind[d, 0, 4 + i, 8:24, :], store_wind_pack(d))

    ex0.wait_recv()
    for x in range(-3, BX + 3):
        b0[1, x + 3] = unpack0(zr0, x, 32)

    def solve(number, base, result):
        c0 = OMEGA / 6.0
        mask_a, mask_h = masks0(place, -4, 24)
        for x in range(-2, BX + 2):
            weight = slab_weight(place, x, BX)
            for t, (c, s) in enumerate(six0(b0, x + 3, 4, 24)):
                value = (1.0 + KEEP) * c0 * c + SIXTH * c0 * s
                v0[t, x + 3, 4:28, :] = scaled(value, (mask_a, mask_h)[t], weight)
        for i in range(6):
            pair = None
            for x in (2 * i, 2 * i + 1):
                ((c, s),) = six0(v0, x + 3, 8, 16, rim=False)
                r = b0[0, x + 3, 8:24, :] - (6.0 * c - s)
                pair = r if pair is None else pair + r
            rows0[i] = pair
        halves = [rows0[i, pl.ds(0, 8, stride=2), :] + rows0[i, pl.ds(1, 8, stride=2), :] for i in range(6)]
        source = dot(jnp.concatenate(halves, axis=0), m_down0[...])

        lane8 = lanes(8)
        low = jnp.zeros((8, 128), jnp.float32)
        high = jnp.zeros((8, 128), jnp.float32)
        for i in range(6):
            block = source[8 * i : 8 * i + 8, :]
            s1[number, i] = block
            l1[number, 4 + i, 8:16, :] = block
            group = (lane8 >= 8 * i) & (lane8 < 8 * i + 8)
            low = jnp.where(group, pltpu.roll(block, 8 * i, 1) if i else block, low)
            high = jnp.where(group, pltpu.roll(block, (8 * i - 56) % 128, 1), high)
        zs1[number, 0] = high
        zs1[number, 1] = low
        ex1 = level1_exchange(number, base)
        ex1.start()
        if number == 0:
            exw.start()
        (ex0 if number == 0 else exf).wait_send()
        ex1.wait_recv()
        lane24 = lanes(24)
        for x in range(-4, 10):
            dx, i = (0, x) if 0 <= x < 6 else ((-1, x + 6) if x < 0 else (1, x - 6))
            left = pltpu.roll(zr1[number, 0, dx + 1], (120 - 8 * i) % 128, 1)
            right = pltpu.roll(zr1[number, 1, dx + 1], (64 - 8 * i) % 128, 1)
            b1[x + 4] = jnp.where(
                lane24 < 64,
                l1[number, x + 4],
                jnp.where(lane24 < 72, right, jnp.where(lane24 >= 120, left, 0.0)),
            )
        w1 = 0.25
        c1 = OMEGA / (6.0 * w1)
        inside = row_mask(place, -4, 16, 8)
        lane16 = lanes(16)
        mask1 = (inside & ((lane16 < 64) | rim_lanes(place, 16, 64, 72))).astype(jnp.float32)
        for x in range(-3, 9):
            c, s = six1(b1, x + 4, 4, 16)
            value = (1.0 + KEEP) * c1 * c + SIXTH * c1 * s
            v1[x + 4, 4:20, :] = scaled(value, mask1, slab_weight(place, x, 6))
        pairs = []
        for i in range(3):
            pair = None
            for x in (2 * i, 2 * i + 1):
                c, s = six1(v1, x + 4, 8, 8)
                r = b1[x + 4, 8:16, :] - w1 * (6.0 * c - s)
                pair = r if pair is None else pair + r
            pairs.append(pair)
        rows2[...] = dot(jnp.concatenate(pairs, axis=1), m_down1[...])
        gathered[number, 2, 1, 2] = rows2[pl.ds(0, 4, stride=2), :] + rows2[pl.ds(1, 4, stride=2), :]

        exa, exb = coarse_exchanges(number, base + 26)
        exa.start()
        ex1.wait_send()
        exa.wait_recv()
        exb.start()
        exb.wait_recv()
        for az in range(3):
            for ax in range(5):
                for ay in range(5):
                    merged[az, ax, 4 * ay : 4 * ay + 4, :] = gathered[number, ay, az, ax]
        for x in range(-5, 8):
            ax, i = (x + 6) // 3, (x + 6) % 3
            parts = [
                pltpu.roll(merged[az, ax], (to - 32 * i) % 128, 1) if (to - 32 * i) % 128 else merged[az, ax]
                for az, to in ((0, 96), (1, 0), (2, 32))
            ]
            c2[x + 5] = jnp.where(
                lane24 < 32,
                parts[1],
                jnp.where(lane24 < 40, parts[2], jnp.where(lane24 >= 120, parts[0], 0.0)),
            )
        w2 = 0.0625
        c2_scale = OMEGA / (6.0 * w2)
        inside = row_mask(place, -6, 16, 4)
        mask2 = (inside & ((lane16 < 32) | rim_lanes(place, 16, 32, 40))).astype(jnp.float32)
        for x in range(-4, 7):
            c, s = six1(c2, x + 5, 2, 16)
            value = (1.0 + KEEP) * c2_scale * c + SIXTH * c2_scale * s
            e2a[x + 5, 2:18, :] = scaled(value, mask2, slab_weight(place, x, 3))
        source_ref, target = e2a, e2b
        for reach in (3, 2):
            for x in range(-reach, 3 + reach):
                c, s = six1(source_ref, x + 5, 2, 16)
                value = KEEP * c + SIXTH * s + c2_scale * c2[x + 5, 2:18, :]
                target[x + 5, 2:18, :] = scaled(value, mask2, slab_weight(place, x, 3))
            source_ref, target = target, source_ref

        spread = dot(
            jnp.concatenate([source_ref[x + 5, 6:14, :] for x in range(-2, 5)], axis=0), m_up1[...]
        )
        for j in range(7):
            value = spread[8 * j : 8 * j + 8, :]
            up1[j, pl.ds(0, 8, stride=2), :] = value
            up1[j, pl.ds(1, 8, stride=2), :] = value
        for x in range(-3, 9):
            v1[x + 4, 4:20, :] += scaled(up1[(x + 4) // 2], mask1, slab_weight(place, x, 6))
        for x in range(-2, 8):
            c, s = six1(v1, x + 4, 4, 16)
            value = KEEP * c + SIXTH * s + c1 * b1[x + 4, 4:20, :]
            up0[0, x + 2, 4:20, :] = scaled(value, mask1, slab_weight(place, x, 6))
        for x in range(-1, 7):
            c, s = six1(up0.at[0], x + 2, 4, 16)
            value = KEEP * c + SIXTH * s + c1 * b1[x + 4, 4:20, :]
            v1[x + 4, 4:20, :] = scaled(value, mask1, slab_weight(place, x, 6))

        spread = dot(
            jnp.concatenate([v1[x + 4, 6:22, :] for x in range(-1, 7)], axis=0), m_up0[...]
        )
        for j in range(8):
            for t in range(2):
                value = spread[16 * j : 16 * j + 12, 128 * t : 128 * t + 128]
                up0[t, j, pl.ds(0, 12, stride=2), :] = value
                up0[t, j, pl.ds(1, 12, stride=2), :] = value
        for x in range(-2, BX + 2):
            weight = slab_weight(place, x, BX)
            for t in range(2):
                v0[t, x + 3, 4:28, :] += scaled(
                    up0[t, (x + 2) // 2, 0:24, :], (mask_a, mask_h)[t], weight
                )
        for x in range(-1, BX + 1):
            weight = slab_weight(place, x, BX)
            for t, (c, s) in enumerate(six0(v0, x + 3, 4, 24)):
                value = KEEP * c + SIXTH * s + c0 * b0[t, x + 3, 4:28, :]
                flux[t // 2, t, x + 1, 4:28, :] = scaled(value, (mask_a, mask_h)[t], weight)
        for x in range(BX):
            ((c, s),) = six0(flux.at[0], x + 1, 8, 16, rim=False)
            result(x, KEEP * c + SIXTH * s + c0 * b0[0, x + 3, 8:24, :])
        return exa, exb

    def keep_first(x, value):
        first[0, x + 6, 16:32, :] = value

    exa, exb = solve(0, 78, keep_first)
    pack0(
        lambda i: first[0, 6 + i, 16:32, :],
        lambda f, l: (zsf.__setitem__(0, l), zsf.__setitem__(1, f)),
    )
    exf.start()
    exa.wait_send()
    exb.wait_send()
    exw.wait_recv()
    exw.wait_send()
    for d in range(3):
        for x in range(-4, BX + 4):
            wind[d, 1, x + 4] = unpack0(zrw.at[:, :, d], x, 32)
    exf.wait_recv()
    for x in range(-6, BX + 6):
        first[1, x + 6, 8:40, :] = unpack0(zrf, x, 32)

    mask_a, mask_h = masks0(place, -8, 32)
    for x in range(-5, BX + 5):
        weight = slab_weight(place, x, BX)
        half = 0.5 if weight is None else 0.5 * weight
        half_a, half_h = mask_a * half, mask_h * half
        i = x + 6
        a, h = first[0, i, 8:40, :], first[1, i, 8:40, :]
        ba, bh = z_back(a, h)
        na, nh = z_next(a, h)
        for t, (b, n, m) in enumerate(((ba, na, half_a), (bh, nh, half_h))):
            velocity[0, t, x + 5, 8:40, :] = (first[t, i + 1, 8:40, :] - first[t, i - 1, 8:40, :]) * m
            velocity[1, t, x + 5, 8:40, :] = (first[t, i, 9:41, :] - first[t, i, 7:39, :]) * m
            velocity[2, t, x + 5, 8:40, :] = (n - b) * m
    mask_a, mask_h = masks0(place, -4, 24)
    for x in range(-4, BX + 4):
        weight = slab_weight(place, x, BX)
        i = x + 5
        half_wind = [[0.5 * wind[e, t, x + 4, 4:28, :] for t in range(2)] for e in range(3)]
        for d in range(3):
            u = velocity.at[d]
            a, h = u[0, i, 12:36, :], u[1, i, 12:36, :]
            ba, bh = z_back(a, h)
            na, nh = z_next(a, h)
            for t, (c, b, n, m) in enumerate(((a, ba, na, mask_a), (h, bh, nh, mask_h))):
                x_low, x_high = u[t, i - 1, 12:36, :], u[t, i + 1, 12:36, :]
                y_low, y_high = u[t, i, 11:35, :], u[t, i, 13:37, :]
                value = (
                    7.0 * c
                    - ((x_low + x_high) + (y_low + y_high) + (b + n))
                    + half_wind[0][t] * (x_high - x_low)
                    + half_wind[1][t] * (y_high - y_low)
                    + half_wind[2][t] * (n - b)
                )
                flux[d, t, x + 4, 4:28, :] = scaled(value, m, weight)
    for x in range(-3, BX + 3):
        weight = slab_weight(place, x, BX)
        i = x + 4
        a, h = flux[2, 0, i, 4:28, :], flux[2, 1, i, 4:28, :]
        ba, bh = z_back(a, h)
        na, nh = z_next(a, h)
        for t, (b, n, m) in enumerate(((ba, na, mask_a), (bh, nh, mask_h))):
            value = (
                (flux[0, t, i + 1, 4:28, :] - flux[0, t, i - 1, 4:28, :])
                + (flux[1, t, i, 5:29, :] - flux[1, t, i, 3:27, :])
                + (n - b)
            ) * -0.5
            b0[t, x + 3, 4:28, :] = scaled(value, m, weight)

    def keep_result(x, value):
        out_ref[x] = value

    exa, exb = solve(1, 122, keep_result)
    exa.wait_send()
    exb.wait_send()


def solution(mesh):
    sizes = tuple(mesh.shape[a] for a in AXES)
    copies = 26 * 3 + 2 * (26 + 18)
    f32 = jnp.float32

    def vmem(*shape):
        return pltpu.VMEM(shape, f32)

    def body(pressure, wind):
        return pl.pallas_call(
            functools.partial(kernel, sizes),
            out_shape=jax.ShapeDtypeStruct((BX, BY, BZ), f32),
            in_specs=[
                pl.BlockSpec(memory_space=pltpu.VMEM),
                pl.BlockSpec(memory_space=pl.ANY),
            ],
            out_specs=pl.BlockSpec(memory_space=pltpu.VMEM),
            scratch_shapes=[
                vmem(2, 18, 32, 128),
                vmem(2, 18, 32, 128),
                vmem(2, 16, 128),
                vmem(2, 3, 32, 128),
                vmem(2, 24, 48, 128),
                vmem(2, 16, 128),
                vmem(2, 3, 32, 128),
                vmem(3, 2, 20, 32, 128),
                vmem(2, 3, 16, 128),
                vmem(2, 3, 3, 32, 128),
                vmem(3, 2, 22, 48, 128),
                vmem(3, 2, 20, 32, 128),
                vmem(2, 6, 8, 128),
                vmem(2, 14, 24, 128),
                vmem(14, 24, 128),
                vmem(14, 24, 128),
                vmem(2, 2, 8, 128),
                vmem(2, 2, 3, 24, 128),
                vmem(2, 5, 3, 5, 4, 128),
                vmem(3, 5, 24, 128),
                vmem(13, 24, 128),
                vmem(13, 24, 128),
                vmem(13, 24, 128),
                vmem(6, 16, 128),
                vmem(8, 128),
                vmem(7, 16, 128),
                vmem(2, 10, 24, 128),
                vmem(128, 128),
                vmem(384, 128),
                vmem(128, 128),
                vmem(128, 256),
                pltpu.SemaphoreType.DMA((copies,)),
                pltpu.SemaphoreType.DMA((copies,)),
                pltpu.SemaphoreType.DMA,
            ],
            compiler_params=pltpu.CompilerParams(
                collective_id=0, has_side_effects=True, vmem_limit_bytes=48 * 1024 * 1024
            ),
            name="schur",
        )(pressure, wind)

    in_specs = (P("gx", "gy", "gz"), P(None, "gx", "gy", "gz"))
    return jax.shard_map(
        body, mesh=mesh, in_specs=in_specs, out_specs=P("gx", "gy", "gz"), check_vma=False
    )
```

time: 487 us -> 61.6 us (0.13)
  the two profiles are of different devices: /device:TPU:281 before, /device:TPU:1 now
where the time goes in v1:
time: 61.6 us; the launch traced here: 61.4 us
  Pallas kernels  58.9 us (96%)
  local copies, waits for them, and re-layouts  2.5 us (4%)
    pallas_call x1, Pallas kernels, body(): pl.pallas_call(functools.partial(kernel, sizes), out_shape=jax.ShapeDtype...  58.9 us
    unnamed x5, local copies, waits for them, and re-layouts  2.5 us

profile of v1, /device:TPU:1, one launch (start us, length us, event | category | flops | bytes accessed | tf_op | source)
XLA Modules:
  0.0 61.4 jit_solution(13920762881113303013)
XLA Ops:
  0.0 0.0 copy-start
  0.0 1.0 %copy-done = f32[3,12,16,128]{3,2,1,0:T(8,128)S(1)} copy-done((f32[3,12,16,128]{3,2,1,0:T(8,128)S(1)}, f32[3,12,16,128]{3,2,1,0:T(8,128)}, u32[]{:S(2)}) %copy-start) | copy-done | bytes 294936
  1.0 0.0 copy-start.1
  1.0 0.9 %copy-done.1 = f32[12,16,128]{2,1,0:T(8,128)S(1)} copy-done((f32[12,16,128]{2,1,0:T(8,128)S(1)}, f32[12,16,128]{2,1,0:T(8,128)}, u32[]{:S(2)}) %copy-start.1) | copy-done | bytes 98328
  1.9 58.9 %schur.1 = f32[12,16,128]{2,1,0:T(8,128)S(1)} custom-call(f32[12,16,128]{2,1,0:T(8,128)S(1)} %copy-done.1, f32[3,12,16,128]{3,2,1,0:T(8,128)S(1)} %copy-done), custom_call_target="tpu_custom_call" | custom-call | tf_op jit(solution)/shard_map/schur/pallas_call | solution.py:564
  60.8 0.6 %copy.4 = f32[12,16,128]{2,1,0:T(8,128)} copy(f32[12,16,128]{2,1,0:T(8,128)S(1)} %schur.1) | data formatting | bytes 196608
Async XLA Ops:
  0.0 1.0 %copy-start = (f32[3,12,16,128]{3,2,1,0:T(8,128)S(1)}, f32[3,12,16,128]{3,2,1,0:T(8,128)}, u32[]{:S(2)}) copy-start(f32[3,12,16,128]{3,2,1,0:T(8,128)} %w_ref.1) | copy-start | bytes 884740
  1.0 0.9 %copy-start.1 = (f32[12,16,128]{2,1,0:T(8,128)S(1)}, f32[12,16,128]{2,1,0:T(8,128)}, u32[]{:S(2)}) copy-start(f32[12,16,128]{2,1,0:T(8,128)} %p_ref.1) | copy-start | bytes 294916

commit v2 on v1

v2 whole, which is shorter than its diff:
```python
import functools

import jax
import jax.numpy as jnp
from jax import lax
from jax.experimental import pallas as pl
from jax.experimental.pallas import tpu as pltpu
from jax.sharding import PartitionSpec as P

MESH = pl.DeviceIdType.MESH
AXES = ("gx", "gy", "gz")
BX, BY, BZ = 12, 16, 128
OMEGA = 0.8
KEEP = 1.0 - OMEGA
SIXTH = OMEGA / 6.0

AROUND = [
    (dx, dy, dz)
    for dz in (0, 1, -1)
    for dx in (0, 1, -1)
    for dy in (0, 1, -1)
    if (dx, dy, dz) != (0, 0, 0)
]
AROUND.sort(key=lambda d: -(abs(d[0]) + abs(d[1]) + abs(d[2])))

NEAR = [d for d in AROUND if sum(map(abs, d)) <= 2]


def coarse_offsets(far_edges):
    out = []
    for dx in range(-2, 3):
        for dy in range(-2, 3):
            for dz in (-1, 0, 1):
                shape = (abs(dx), abs(dy), abs(dz))
                if shape[:2] in ((0, 0), (0, 1), (1, 0), (1, 1), (0, 2), (2, 0), (2, 1)):
                    keep = shape != (0, 0, 0)
                else:
                    keep = far_edges and shape[:2] == (1, 2)
                if keep:
                    out.append((dx, dy, dz))
    return sorted(out, key=lambda d: -sum(map(abs, d)))


COARSE = (coarse_offsets(True), coarse_offsets(False))
GREETED = coarse_offsets(True)


def part(delta, count, width):
    if delta == 0:
        return 0, 0, count
    if delta > 0:
        return count - width, -width, width
    return 0, count, width


class Place:
    def __init__(self, sizes):
        self.sizes = sizes
        self.at = [lax.axis_index(a) for a in AXES]
        self.has = []
        for g, n in zip(self.at, sizes):
            self.has.append({d: (g + d >= 0) & (g + d < n) for d in (-2, -1, 1, 2)})

    def exists(self, offset):
        found = None
        for table, d in zip(self.has, offset):
            if d:
                found = table[d] if found is None else found & table[d]
        return found

    def device(self, offset):
        return tuple(
            lax.rem(g + (d + n), n) if d else g for g, d, n in zip(self.at, offset, self.sizes)
        )


class Exchange:
    def __init__(self, place, copies, send_sems, recv_sems, base):
        self.place, self.items = place, []
        for k, (offset, src, dst) in enumerate(copies):
            copy = pltpu.make_async_remote_copy(
                src_ref=src,
                dst_ref=dst,
                send_sem=send_sems.at[base + k],
                recv_sem=recv_sems.at[base + k],
                device_id=place.device(offset),
                device_id_type=MESH,
            )
            self.items.append((offset, copy))

    def start(self):
        for offset, copy in self.items:
            pl.when(self.place.exists(offset))(copy.start)

    def wait_recv(self):
        for offset, copy in self.items:
            pl.when(self.place.exists(tuple(-d for d in offset)))(copy.wait_recv)

    def wait_send(self):
        for offset, copy in self.items:
            pl.when(self.place.exists(offset))(copy.wait_send)


def lanes(rows):
    return lax.broadcasted_iota(jnp.int32, (rows, 128), 1)


def row_mask(place, first_row, rows, extent):
    y = first_row + lax.broadcasted_iota(jnp.int32, (rows, 128), 0)
    low = jnp.where(place.has[1][-1], -64, 0)
    high = jnp.where(place.has[1][1], 64, extent)
    return (y >= low) & (y < high)


def rim_lanes(place, rows, start, right_end):
    lane = lanes(rows)
    right_stop = jnp.where(place.has[2][1], right_end, 0)
    left_start = jnp.where(place.has[2][-1], 120, 128)
    return ((lane >= start) & (lane < right_stop)) | (lane >= left_start)


def slab_weight(place, x, extent):
    if x < 0:
        return place.has[0][-1].astype(jnp.float32)
    if x >= extent:
        return place.has[0][1].astype(jnp.float32)
    return None


def z_back(a, h):
    lane0 = lanes(a.shape[0]) == 0
    ra, rh = pltpu.roll(a, 1, 1), pltpu.roll(h, 1, 1)
    return jnp.where(lane0, rh, ra), jnp.where(lane0, ra, rh)


def z_next(a, h):
    lane127 = lanes(a.shape[0]) == 127
    ra, rh = pltpu.roll(a, 127, 1), pltpu.roll(h, 127, 1)
    return jnp.where(lane127, rh, ra), jnp.where(lane127, ra, rh)


def masks0(place, first_row, rows):
    inner = row_mask(place, first_row, rows, BY)
    rim = inner & rim_lanes(place, rows, 0, 8)
    return inner.astype(jnp.float32), rim.astype(jnp.float32)


def scaled(value, mask, weight):
    value = value * mask
    return value if weight is None else value * weight


def six0(ref, i, r, n, rim=True):
    a, h = ref[0, i, r : r + n, :], ref[1, i, r : r + n, :]
    ba, bh = z_back(a, h)
    na, nh = z_next(a, h)
    out = []
    for t, (c, b, f) in enumerate(((a, ba, na), (h, bh, nh))):
        if t and not rim:
            break
        s = (
            (ref[t, i - 1, r : r + n, :] + ref[t, i + 1, r : r + n, :])
            + (ref[t, i, r - 1 : r - 1 + n, :] + ref[t, i, r + 1 : r + 1 + n, :])
            + (b + f)
        )
        out.append((c, s))
    return out


def six1(ref, i, r, n):
    c = ref[i, r : r + n, :]
    s = (
        (ref[i - 1, r : r + n, :] + ref[i + 1, r : r + n, :])
        + (ref[i, r - 1 : r - 1 + n, :] + ref[i, r + 1 : r + 1 + n, :])
        + (pltpu.roll(c, 1, 1) + pltpu.roll(c, 127, 1))
    )
    return c, s


def pick(a, m):
    high = a.astype(jnp.bfloat16)
    low = (a - high.astype(jnp.float32)).astype(jnp.bfloat16)
    return jnp.dot(high, m, preferred_element_type=jnp.float32) + jnp.dot(
        low, m, preferred_element_type=jnp.float32
    )


def turn(value, shift):
    shift %= 128
    return pltpu.roll(value, shift, 1) if shift else value


def pack0(load, store):
    lane = lanes(BY)
    first = jnp.zeros((BY, 128), jnp.float32)
    last = jnp.zeros((BY, 128), jnp.float32)
    for i in range(BX):
        turned = turn(load(i), 8 * i)
        first = jnp.where((lane >= 8 * i) & (lane < 8 * i + 8), turned, first)
        at = (8 * i - 8) % 128
        last = jnp.where((lane >= at) & (lane < at + 8), turned, last)
    store(first, last)


def beside(x, count):
    return (0, x) if 0 <= x < count else ((-1, x + count) if x < 0 else (1, x - count))


def unpack0(land, x, rows):
    dx, i = beside(x, BX)
    left, right = turn(land[0, dx + 1], -8 * i), turn(land[1, dx + 1], -8 * i)
    lane = lanes(rows)
    return jnp.where(lane < 8, right, jnp.where(lane >= 120, left, 0.0))


def rim_copies(source, land, offsets):
    out = []
    for offset in offsets:
        dx, dy, dz = offset
        if dz == 0:
            continue
        y0, yd, ny = part(dy, BY, 8)
        side = 0 if dz > 0 else 1
        out.append((offset, source(side, y0, ny), land(side, 1 - dx, yd, ny)))
    return out


def block_copies(source, land, h, offsets):
    out = []
    for offset in offsets:
        dx, dy, dz = offset
        if dz != 0:
            continue
        x0, xd, nx = part(dx, BX, h)
        y0, yd, ny = part(dy, BY, 8)
        out.append((offset, source(x0, nx, y0, ny), land(xd, nx, yd, ny)))
    return out


def ordered(copies):
    return sorted(copies, key=lambda c: -sum(abs(d) for d in c[0]))


def clear_around(ref, lead_x, lead_y, count_y):
    nx, ny = ref.shape[0], ref.shape[1]
    ref[0:lead_x] = jnp.zeros((lead_x, ny, 128), jnp.float32)
    ref[lead_x + BX : nx] = jnp.zeros((nx - lead_x - BX, ny, 128), jnp.float32)
    ref[lead_x : lead_x + BX, 0:lead_y, :] = jnp.zeros((BX, lead_y, 128), jnp.float32)
    end = lead_y + count_y
    ref[lead_x : lead_x + BX, end:ny, :] = jnp.zeros((BX, ny - end, 128), jnp.float32)


def clear(*refs):
    for ref in refs:
        ref[...] = jnp.zeros(ref.shape, ref.dtype)


def kernel(
    sizes, p_ref, w_ref, out_ref,
    b0, v0, t0, zs0, zr0, wind, zsw, zrw, velocity, flux,
    vp, zsv, zrv,
    bv, zsb, zrb, s1, l1, zs1, zr1, b1, v1, t1,
    gathered, merged, c2, e2a, e2b,
    rows0, rows2, up1, up0, m_down0, m_down1, m_up1, m_up0,
    send_sems, recv_sems, load_sems,
):
    place = Place(sizes)
    load_p = pltpu.make_async_copy(
        p_ref, b0.at[0, pl.ds(8, BX), pl.ds(16, BY), :], load_sems.at[0])
    load_w = pltpu.make_async_copy(
        w_ref, wind.at[:, 0, pl.ds(3, BX), pl.ds(8, BY), :], load_sems.at[1])
    load_p.start()
    load_w.start()

    clear_around(b0.at[0], 8, 16, BY)
    for d in range(3):
        clear_around(wind.at[d, 0], 3, 8, BY)
    clear(zr0, zrw, vp, zrv, bv, zrb, l1, zr1, gathered)

    barrier = pltpu.get_barrier_semaphore()
    total = jnp.int32(0)
    for offset in GREETED:
        there = place.exists(offset)
        total = total + there.astype(jnp.int32)

        def greet(offset=offset):
            pl.semaphore_signal(
                barrier, inc=1, device_id=place.device(offset), device_id_type=MESH
            )

        pl.when(there)(greet)

    def storer(ref):
        def store(f, l):
            ref[0] = l
            ref[1] = f
        return store

    clear(b0.at[1], v0, t0, rows0)
    load_p.wait()
    pack0(lambda i: b0[0, 8 + i, 16:32, :], storer(zs0))

    used = [0]

    def exchange(copies):
        base = used[0]
        used[0] += len(copies)
        return Exchange(place, ordered(copies), send_sems, recv_sems, base)

    def b0_block(x, nx, y, ny):
        return b0.at[0, pl.ds(x + 8, nx), pl.ds(y + 16, ny), :]

    def wind_block(x, nx, y, ny):
        return wind.at[:, 0, pl.ds(x + 3, nx), pl.ds(y + 8, ny), :]

    def vp_block(x, nx, y, ny):
        return vp.at[pl.ds(x + 2, nx), pl.ds(y + 16, ny), :]

    ex0 = exchange(
        block_copies(b0_block, b0_block, 8, AROUND)
        + rim_copies(
            lambda s, y, ny: zs0.at[s, pl.ds(y, ny), :],
            lambda s, dx, y, ny: zr0.at[s, dx, pl.ds(y + 8, ny), :], AROUND))
    exw = exchange(
        block_copies(wind_block, wind_block, 3, AROUND)
        + rim_copies(
            lambda s, y, ny: zsw.at[s, :, pl.ds(y, ny), :],
            lambda s, dx, y, ny: zrw.at[s, dx, :, pl.ds(y + 8, ny), :], AROUND))
    exv = exchange(
        block_copies(vp_block, vp_block, 2, NEAR)
        + rim_copies(
            lambda s, y, ny: zsv.at[s, pl.ds(y, ny), :],
            lambda s, dx, y, ny: zrv.at[s, dx, pl.ds(y + 8, ny), :], NEAR))

    def bv_copies():
        out = []
        for offset in AROUND:
            dx, dy, dz = offset
            if dz == 0:
                out.append((
                    offset, bv.at[pl.ds(6, 6), pl.ds(16, 8), :],
                    bv.at[pl.ds(6 - 6 * dx, 6), pl.ds(16 - 8 * dy, 8), :]))
            else:
                side = 0 if dz > 0 else 1
                out.append((
                    offset, zsb.at[side], zrb.at[side, 1 - dx, pl.ds(8 - 8 * dy, 8), :]))
        return out

    def level1_copies():
        out = []
        for offset in AROUND:
            dx, dy, dz = offset
            if dz == 0:
                x0, xd, nx = part(dx, 6, 4)
                out.append((
                    offset, s1.at[pl.ds(x0, nx)],
                    l1.at[pl.ds(xd + 4, nx), pl.ds(8 - 8 * dy, 8), :]))
            else:
                side = 0 if dz > 0 else 1
                out.append((
                    offset, zs1.at[side], zr1.at[side, 1 - dx, pl.ds(8 - 8 * dy, 8), :]))
        return out

    def coarse_copies(number):
        return [
            (d, gathered.at[number, 2, 1, 2], gathered.at[number, 2 - d[1], 1 - d[2], 2 - d[0]])
            for d in COARSE[number]
        ]

    exb = exchange(bv_copies())
    ex1 = exchange(level1_copies())
    ex2 = [exchange(coarse_copies(0)), exchange(coarse_copies(1))]

    pl.semaphore_wait(barrier, total)
    ex0.start()

    load_w.wait()
    for d in range(3):
        pack0(lambda i: wind[d, 0, 3 + i, 8:24, :], storer(zsw.at[:, d]))
    exw.start()

    clear(velocity, flux, b1, v1, t1, merged, c2, e2a, e2b, rows2, up1, up0)

    bf16 = jnp.bfloat16
    k = lax.broadcasted_iota(jnp.int32, (128, 128), 0)
    l = lax.broadcasted_iota(jnp.int32, (128, 128), 1)
    eighth = jnp.float32(0.125)
    m_down0[0:128, :] = jnp.where(k // 2 == l, eighth, 0.0).astype(bf16)
    m_down0[128:256, :] = jnp.where(
        ((k < 8) | (k >= 120)) & (k // 2 + 64 == l), eighth, 0.0).astype(bf16)
    for i in range(3):
        m_down1[i * 128 : i * 128 + 128, :] = jnp.where(
            (l // 32 == i) & (k // 2 == l % 32), eighth, 0.0).astype(bf16)
    m_up1[...] = jnp.where(
        ((l < 72) & (k == l // 2)) | ((l >= 120) & (k == 64 + l // 2)), 1.0, 0.0).astype(bf16)
    m_up0[:, 0:128] = jnp.where(k == l // 2, 1.0, 0.0).astype(bf16)
    m_up0[:, 128:256] = jnp.where(
        ((l < 8) | (l >= 120)) & (k == 64 + l // 2), 1.0, 0.0).astype(bf16)

    c0 = OMEGA / 6.0
    w1 = 0.25
    c1 = OMEGA / (6.0 * w1)
    w2 = 0.0625
    c2s = OMEGA / (6.0 * w2)
    lane8, lane16, lane24, lane40 = lanes(8), lanes(16), lanes(24), lanes(40)
    m32a, m32h = masks0(place, -8, 32)
    m24a, m24h = masks0(place, -4, 24)
    mask32, mask24 = (m32a, m32h), (m24a, m24h)

    def level1_mask(first_row, rows):
        lane = lanes(rows)
        inside = row_mask(place, first_row, rows, 8)
        return (inside & ((lane < 64) | rim_lanes(place, rows, 64, 72))).astype(jnp.float32)

    def first_two0(reach, r, n, masks):
        for x in range(-reach, BX + reach):
            weight = slab_weight(place, x, BX)
            for t, (c, s) in enumerate(six0(b0, x + 8, r, n)):
                value = (1.0 + KEEP) * c0 * c + SIXTH * c0 * s
                v0[t, x + 8, r : r + n, :] = scaled(value, masks[t], weight)

    def down1_and_send(number, r, n):
        pairs = []
        for i in range(3):
            pair = None
            for x in (2 * i, 2 * i + 1):
                c, s = six1(v1, x + 6, 16, 8)
                res = b1[x + 6, 16:24, :] - w1 * (6.0 * c - s)
                pair = res if pair is None else pair + res
            pairs.append(jnp.where(lane8 < 64, pair, 0.0))
        rows2[...] = pick(jnp.concatenate(pairs, axis=1), m_down1[...])
        gathered[number, 2, 1, 2] = (
            rows2[pl.ds(0, 4, stride=2), :] + rows2[pl.ds(1, 4, stride=2), :])
        ex2[number].start()

    def coarse(number, reach):
        for az in range(3):
            for ax in range(5):
                for ay in range(5):
                    merged[az, ax, 4 * ay : 4 * ay + 4, :] = gathered[number, ay, az, ax]
        for x in range(-reach - 3, 3 + reach + 3):
            ax, i = (x + 6) // 3, (x + 6) % 3
            left = turn(merged[0, ax], 96 - 32 * i)
            own = turn(merged[1, ax], -32 * i)
            right = turn(merged[2, ax], 32 - 32 * i)
            c2[x + 6] = jnp.where(
                lane24 < 32, own, jnp.where(lane24 < 40, right, jnp.where(lane24 >= 120, left, 0.0)))
        inside = row_mask(place, -6, 16, 4)
        mask2 = (inside & ((lane16 < 32) | rim_lanes(place, 16, 32, 40))).astype(jnp.float32)
        for x in range(-reach - 2, 3 + reach + 2):
            c, s = six1(c2, x + 6, 2, 16)
            value = (1.0 + KEEP) * c2s * c + SIXTH * c2s * s
            e2a[x + 6, 2:18, :] = scaled(value, mask2, slab_weight(place, x, 3))
        here, there = e2a, e2b
        for more in (1, 0):
            for x in range(-reach - more, 3 + reach + more):
                c, s = six1(here, x + 6, 2, 16)
                value = KEEP * c + SIXTH * s + c2s * c2[x + 6, 2:18, :]
                there[x + 6, 2:18, :] = scaled(value, mask2, slab_weight(place, x, 3))
            here, there = there, here
        return here

    def spread1(here, reach, y, n):
        slabs = 3 + 2 * reach
        spread = pick(
            jnp.concatenate([here[x - reach + 6, y + 8 : y + 8 + n, :] for x in range(slabs)], axis=0),
            m_up1[...])
        for j in range(slabs):
            value = spread[n * j : n * j + n, :]
            up1[j, pl.ds(0, n, stride=2), :] = value
            up1[j, pl.ds(1, n, stride=2), :] = value

    def last_two1(reach, r, n, mask):
        for x in range(-reach - 1, 6 + reach + 1):
            c, s = six1(v1, x + 6, r, n)
            value = KEEP * c + SIXTH * s + c1 * b1[x + 6, r : r + n, :]
            t1[x + 6, r : r + n, :] = scaled(value, mask, slab_weight(place, x, 6))
        for x in range(-reach, 6 + reach):
            c, s = six1(t1, x + 6, r, n)
            value = KEEP * c + SIXTH * s + c1 * b1[x + 6, r : r + n, :]
            v1[x + 6, r : r + n, :] = scaled(value, mask, slab_weight(place, x, 6))

    def spread0(reach, n):
        y = -(n - 8) // 2
        slabs = 6 + 2 * reach
        spread = pick(
            jnp.concatenate(
                [v1[x - reach + 6, y + 16 : y + 32, :] for x in range(slabs)], axis=0),
            m_up0[...])
        for j in range(slabs):
            for t in range(2):
                value = spread[16 * j : 16 * j + n, 128 * t : 128 * t + 128]
                up0[t, j, pl.ds(0, n, stride=2), :] = value
                up0[t, j, pl.ds(1, n, stride=2), :] = value

    ex0.wait_recv()
    for x in range(-8, BX + 8):
        b0[1, x + 8, 8:40, :] = unpack0(zr0, x, 32)
    first_two0(7, 8, 32, mask32)
    for i in range(10):
        pair = [None, None]
        for x in (2 * i - 4, 2 * i - 3):
            for t, (c, s) in enumerate(six0(v0, x + 8, 12, 24)):
                res = b0[t, x + 8, 12:36, :] - (6.0 * c - s)
                pair[t] = res if pair[t] is None else pair[t] + res
        for t in range(2):
            rows0[t, i, 0:24, :] = pair[t]
    cells = [
        jnp.concatenate(
            [rows0[t, i, pl.ds(0, 16, stride=2), :] + rows0[t, i, pl.ds(1, 16, stride=2), :]
             for t in range(2)], axis=1)
        for i in range(10)
    ]
    source = pick(jnp.concatenate(cells, axis=0), m_down0[...])
    mask = level1_mask(-2, 16)
    for x in range(-2, 8):
        b1[x + 6, 14:30, :] = scaled(
            source[16 * (x + 2) : 16 * (x + 2) + 16, :], mask, slab_weight(place, x, 6))
    for x in range(-1, 7):
        c, s = six1(b1, x + 6, 14, 16)
        value = (1.0 + KEEP) * c1 * c + SIXTH * c1 * s
        v1[x + 6, 14:30, :] = scaled(value, mask, slab_weight(place, x, 6))
    down1_and_send(0, 14, 16)

    low = jnp.zeros((8, 128), jnp.float32)
    high = jnp.zeros((8, 128), jnp.float32)
    for i in range(6):
        block_b, block_v = b1[i + 6, 16:24, :], v1[i + 6, 16:24, :]
        bv[i + 6, 16:24, :] = jnp.where(lane8 < 64, block_b, pltpu.roll(block_v, 64, 1))
        for block, lead in ((block_b, 0), (block_v, 64)):
            group = (lane8 >= lead + 8 * i) & (lane8 < lead + 8 * i + 8)
            low = jnp.where(group, turn(block, lead + 8 * i), low)
            high = jnp.where(group, turn(block, lead + 8 * i - 56), high)
    zsb[0] = high
    zsb[1] = low
    exb.start()
    ex0.wait_send()
    exw.wait_recv()
    for d in range(3):
        for x in range(-3, BX + 3):
            wind[d, 1, x + 3] = unpack0(zrw.at[:, :, d], x, 32)
    exw.wait_send()
    ex2[0].wait_recv()
    here = coarse(0, 3)
    spread1(here, 3, -4, 16)
    exb.wait_recv()
    mask = level1_mask(-8, 24)
    for x in range(-6, 12):
        dx, i = beside(x, 6)
        near = bv[x + 6, 8:32, :]
        left, right = zrb[0, dx + 1], zrb[1, dx + 1]
        for lead, ref in ((0, b1), (64, v1)):
            value = jnp.where(
                lane24 < 64, turn(near, -lead),
                jnp.where(lane24 < 72, turn(right, 64 - 8 * i - lead),
                          jnp.where(lane24 >= 120, turn(left, 120 - 8 * i - lead), 0.0)))
            if ref is v1:
                value = value + scaled(
                    up1[(x + 6) // 2, 0:24, :], mask, slab_weight(place, x, 6))
            ref[x + 6, 8:32, :] = value
    last_two1(4, 8, 24, mask)
    spread0(4, 16)
    for x in range(-7, BX + 7):
        weight = slab_weight(place, x, BX)
        for t in range(2):
            v0[t, x + 8, 8:40, :] += scaled(up0[t, (x + 8) // 2], mask32[t], weight)
    for x in range(-6, BX + 6):
        weight = slab_weight(place, x, BX)
        for t, (c, s) in enumerate(six0(v0, x + 8, 8, 32)):
            value = KEEP * c + SIXTH * s + c0 * b0[t, x + 8, 8:40, :]
            t0[t, x + 8, 8:40, :] = scaled(value, mask32[t], weight)
    for x in range(-5, BX + 5):
        weight = slab_weight(place, x, BX)
        for t, (c, s) in enumerate(six0(t0, x + 8, 8, 32)):
            value = KEEP * c + SIXTH * s + c0 * b0[t, x + 8, 8:40, :]
            v0[t, x + 8, 8:40, :] = scaled(value, mask32[t], weight)
    first = v0

    for x in range(-4, BX + 4):
        weight = slab_weight(place, x, BX)
        half = 0.5 if weight is None else 0.5 * weight
        i = x + 8
        a, h = first[0, i, 12:36, :], first[1, i, 12:36, :]
        ba, bh = z_back(a, h)
        na, nh = z_next(a, h)
        for t, (b, n) in enumerate(((ba, na), (bh, nh))):
            m = mask24[t] * half
            velocity[0, t, x + 4, 12:36, :] = (first[t, i + 1, 12:36, :] - first[t, i - 1, 12:36, :]) * m
            velocity[1, t, x + 4, 12:36, :] = (first[t, i, 13:37, :] - first[t, i, 11:35, :]) * m
            velocity[2, t, x + 4, 12:36, :] = (n - b) * m
    for x in range(-3, BX + 3):
        weight = slab_weight(place, x, BX)
        i = x + 4
        half_wind = [[0.5 * wind[e, t, x + 3, 4:28, :] for t in range(2)] for e in range(3)]
        for d in range(3):
            u = velocity.at[d]
            a, h = u[0, i, 12:36, :], u[1, i, 12:36, :]
            ba, bh = z_back(a, h)
            na, nh = z_next(a, h)
            for t, (c, b, n) in enumerate(((a, ba, na), (h, bh, nh))):
                x_low, x_high = u[t, i - 1, 12:36, :], u[t, i + 1, 12:36, :]
                y_low, y_high = u[t, i, 11:35, :], u[t, i, 13:37, :]
                value = (
                    7.0 * c
                    - ((x_low + x_high) + (y_low + y_high) + (b + n))
                    + half_wind[0][t] * (x_high - x_low)
                    + half_wind[1][t] * (y_high - y_low)
                    + half_wind[2][t] * (n - b)
                )
                flux[d, t, x + 3, 4:28, :] = scaled(value, mask24[t], weight)
    for x in range(-2, BX + 2):
        weight = slab_weight(place, x, BX)
        i = x + 3
        a, h = flux[2, 0, i, 4:28, :], flux[2, 1, i, 4:28, :]
        ba, bh = z_back(a, h)
        na, nh = z_next(a, h)
        for t, (b, n) in enumerate(((ba, na), (bh, nh))):
            value = (
                (flux[0, t, i + 1, 4:28, :] - flux[0, t, i - 1, 4:28, :])
                + (flux[1, t, i, 5:29, :] - flux[1, t, i, 3:27, :])
                + (n - b)
            ) * -0.5
            b0[t, x + 8, 12:36, :] = scaled(value, mask24[t], weight)

    first_two0(1, 12, 24, mask24)
    for i in range(6):
        pair = None
        for x in (2 * i, 2 * i + 1):
            ((c, s),) = six0(v0, x + 8, 16, 16, rim=False)
            res = b0[0, x + 8, 16:32, :] - (6.0 * c - s)
            pair = res if pair is None else pair + res
        rows0[0, i, 0:16, :] = pair
    cells = [rows0[0, i, pl.ds(0, 8, stride=2), :] + rows0[0, i, pl.ds(1, 8, stride=2), :] for i in range(6)]
    source = pick(jnp.concatenate(cells, axis=0), m_down0[0:128, :])
    low = jnp.zeros((8, 128), jnp.float32)
    high = jnp.zeros((8, 128), jnp.float32)
    for i in range(6):
        block = source[8 * i : 8 * i + 8, :]
        s1[i] = block
        l1[4 + i, 8:16, :] = block
        group = (lane8 >= 8 * i) & (lane8 < 8 * i + 8)
        low = jnp.where(group, turn(block, 8 * i), low)
        high = jnp.where(group, turn(block, 8 * i - 56), high)
    zs1[0] = high
    zs1[1] = low
    ex1.start()
    for x in range(BX):
        vp[x + 2, 16:32, :] = v0[0, x + 8, 16:32, :]
    pack0(lambda i: v0[0, 8 + i, 16:32, :], storer(zsv))
    exv.start()
    ex2[0].wait_send()
    exb.wait_send()
    ex1.wait_recv()
    for x in range(-4, 10):
        dx, i = beside(x, 6)
        b1[x + 6, 8:32, :] = jnp.where(
            lane24 < 64, l1[x + 4],
            jnp.where(lane24 < 72, turn(zr1[1, dx + 1], 64 - 8 * i),
                      jnp.where(lane24 >= 120, turn(zr1[0, dx + 1], 120 - 8 * i), 0.0)))
    mask = level1_mask(-4, 16)
    for x in range(-3, 9):
        c, s = six1(b1, x + 6, 12, 16)
        value = (1.0 + KEEP) * c1 * c + SIXTH * c1 * s
        v1[x + 6, 12:28, :] = scaled(value, mask, slab_weight(place, x, 6))
    down1_and_send(1, 12, 16)
    ex1.wait_send()
    exv.wait_send()
    exv.wait_recv()
    for x in range(-2, BX + 2):
        v0[0, x + 8, 12:36, :] = vp[x + 2, 12:36, :]
        v0[1, x + 8, 8:40, :] = unpack0(zrv, x, 32)
    ex2[1].wait_recv()
    here = coarse(1, 2)
    spread1(here, 2, -2, 8)
    for x in range(-3, 9):
        v1[x + 6, 12:28, :] += scaled(up1[(x + 4) // 2, 0:16, :], mask, slab_weight(place, x, 6))
    last_two1(1, 12, 16, mask)
    spread0(1, 12)
    for x in range(-2, BX + 2):
        weight = slab_weight(place, x, BX)
        for t in range(2):
            v0[t, x + 8, 12:36, :] += scaled(up0[t, (x + 2) // 2, 0:24, :], mask24[t], weight)
    for x in range(-1, BX + 1):
        weight = slab_weight(place, x, BX)
        for t, (c, s) in enumerate(six0(v0, x + 8, 12, 24)):
            value = KEEP * c + SIXTH * s + c0 * b0[t, x + 8, 12:36, :]
            t0[t, x + 8, 12:36, :] = scaled(value, mask24[t], weight)
    for x in range(BX):
        ((c, s),) = six0(t0, x + 8, 16, 16, rim=False)
        out_ref[x] = KEEP * c + SIXTH * s + c0 * b0[0, x + 8, 16:32, :]
    ex2[1].wait_send()


def solution(mesh):
    sizes = tuple(mesh.shape[a] for a in AXES)
    copies = 26 * 4 + len(NEAR) + len(COARSE[0]) + len(COARSE[1])
    f32 = jnp.float32
    bf16 = jnp.bfloat16

    def vmem(*shape, dtype=f32):
        return pltpu.VMEM(shape, dtype)

    def body(pressure, wind):
        return pl.pallas_call(
            functools.partial(kernel, sizes),
            out_shape=jax.ShapeDtypeStruct((BX, BY, BZ), f32),
            in_specs=[pl.BlockSpec(memory_space=pl.ANY)] * 2,
            out_specs=pl.BlockSpec(memory_space=pltpu.VMEM),
            scratch_shapes=[
                vmem(2, 28, 48, 128),
                vmem(2, 28, 48, 128),
                vmem(2, 28, 48, 128),
                vmem(2, 16, 128),
                vmem(2, 3, 32, 128),
                vmem(3, 2, 18, 32, 128),
                vmem(2, 3, 16, 128),
                vmem(2, 3, 3, 32, 128),
                vmem(3, 2, 20, 48, 128),
                vmem(3, 2, 18, 32, 128),
                vmem(16, 48, 128),
                vmem(2, 16, 128),
                vmem(2, 3, 32, 128),
                vmem(18, 40, 128),
                vmem(2, 8, 128),
                vmem(2, 3, 24, 128),
                vmem(6, 8, 128),
                vmem(14, 24, 128),
                vmem(2, 8, 128),
                vmem(2, 3, 24, 128),
                vmem(18, 40, 128),
                vmem(18, 40, 128),
                vmem(18, 40, 128),
                vmem(2, 5, 3, 5, 4, 128),
                vmem(3, 5, 24, 128),
                vmem(15, 24, 128),
                vmem(15, 24, 128),
                vmem(15, 24, 128),
                vmem(2, 10, 32, 128),
                vmem(8, 128),
                vmem(9, 32, 128),
                vmem(2, 14, 32, 128),
                vmem(256, 128, dtype=bf16),
                vmem(384, 128, dtype=bf16),
                vmem(128, 128, dtype=bf16),
                vmem(128, 256, dtype=bf16),
                pltpu.SemaphoreType.DMA((copies,)),
                pltpu.SemaphoreType.DMA((copies,)),
                pltpu.SemaphoreType.DMA((2,)),
            ],
            compiler_params=pltpu.CompilerParams(
                collective_id=0, has_side_effects=True, vmem_limit_bytes=67043328
            ),
            name="schur",
        )(pressure, wind)

    in_specs = (P("gx", "gy", "gz"), P(None, "gx", "gy", "gz"))
    return jax.shard_map(
        body, mesh=mesh, in_specs=in_specs, out_specs=P("gx", "gy", "gz"), check_vma=False
    )
```

time: 61.6 us -> 49.6 us (0.81)
  Pallas kernels: 58.9 us -> 47.9 us
  local copies, waits for them, and re-layouts: 2.5 us -> 1.54 us
    pallas_call x1, Pallas kernels: 58.9 us -> 47.9 us  [body(): pl.pallas_call(functools.partial(kernel, sizes), out_shape=jax.ShapeDtype...]
    unnamed x5 -> x1, local copies, waits for them, and re-layouts: 2.5 us -> 1.54 us
where the time goes in v2:
time: 49.6 us; the launch traced here: 49.4 us
  Pallas kernels  47.9 us (97%)
  local copies, waits for them, and re-layouts  1.54 us (3%)
    pallas_call x1, Pallas kernels, body(): pl.pallas_call(functools.partial(kernel, sizes), out_shape=jax.ShapeDtype...  47.9 us
    unnamed x1, local copies, waits for them, and re-layouts  1.54 us

profile of v2, /device:TPU:1, one launch (start us, length us, event | category | flops | bytes accessed | tf_op | source)
XLA Modules:
  0.0 49.4 jit_solution(7404103857877659767)
XLA Ops:
  0.0 47.9 %schur.1 = f32[12,16,128]{2,1,0:T(8,128)} custom-call(f32[12,16,128]{2,1,0:T(8,128)} %p_ref.1, f32[3,12,16,128]{3,2,1,0:T(8,128)} %w_ref.1), custom_call_target="tpu_custom_call" | custom-call | tf_op jit(solution)/shard_map/schur/pallas_call | solution.py:704
  47.9 1.5 %copy.4 = f32[12,16,128]{2,1,0:T(8,128)} copy(f32[12,16,128]{2,1,0:T(8,128)} %schur.1) | data formatting | bytes 196608

commit v3 on v2

--- a/solution.py
+++ b/solution.py
@@ -61,6 +61,25 @@
         for g, n in zip(self.at, sizes):
             self.has.append({d: (g + d >= 0) & (g + d < n) for d in (-2, -1, 1, 2)})
 
+        kinds = []
+        for n in sizes:
+            kinds.append(sorted({
+                tuple(sum(0 <= g + d < n for d in (-k, k)) for k in (1, 2)) for g in range(n)
+            }))
+        self.profiles = [(a, b, c) for a in kinds[0] for b in kinds[1] for c in kinds[2]]
+        self.kinds = kinds
+        self.counts = [
+            [t[-k].astype(jnp.int32) + t[k].astype(jnp.int32) for k in (1, 2)] for t in self.has
+        ]
+
+    def matches(self, profile):
+        found = None
+        for counts, wanted, kinds in zip(self.counts, profile, self.kinds):
+            for c, v, seen in zip(counts, wanted, zip(*kinds)):
+                if len(set(seen)) > 1:
+                    found = (c == v) if found is None else found & (c == v)
+        return True if found is None else found
+
     def exists(self, offset):
         found = None
         for table, d in zip(self.has, offset):
@@ -75,30 +94,47 @@
 
 
 class Exchange:
-    def __init__(self, place, copies, send_sems, recv_sems, base):
+    def __init__(self, place, copies, send_sem, recv_sem, ruler):
         self.place, self.items = place, []
-        for k, (offset, src, dst) in enumerate(copies):
+        self.send_sem, self.recv_sem, self.ruler = send_sem, recv_sem, ruler
+        self.weights = []
+        for offset, src, dst in copies:
             copy = pltpu.make_async_remote_copy(
                 src_ref=src,
                 dst_ref=dst,
-                send_sem=send_sems.at[base + k],
-                recv_sem=recv_sems.at[base + k],
+                send_sem=send_sem,
+                recv_sem=recv_sem,
                 device_id=place.device(offset),
                 device_id_type=MESH,
             )
             self.items.append((offset, copy))
+            units = 1
+            for n in src.shape:
+                units *= n
+            self.weights.append((tuple(abs(d) for d in offset), units // 512))
 
     def start(self):
         for offset, copy in self.items:
             pl.when(self.place.exists(offset))(copy.start)
 
+    def wait(self, sem):
+        for profile in self.place.profiles:
+            total = 0
+            for shape, units in self.weights:
+                share = 8 * units
+                for counts, d in zip(profile, shape):
+                    share = share * counts[d - 1] // 2 if d else share
+                total += share
+            total //= 8
+            if total:
+                rows = self.ruler.at[pl.ds(0, total)]
+                pl.when(self.place.matches(profile))(pltpu.make_async_copy(rows, rows, sem).wait)
+
     def wait_recv(self):
-        for offset, copy in self.items:
-            pl.when(self.place.exists(tuple(-d for d in offset)))(copy.wait_recv)
+        self.wait(self.recv_sem)
 
     def wait_send(self):
-        for offset, copy in self.items:
-            pl.when(self.place.exists(offset))(copy.wait_send)
+        self.wait(self.send_sem)
 
 
 def lanes(rows):
@@ -190,11 +226,11 @@
     return pltpu.roll(value, shift, 1) if shift else value
 
 
-def pack0(load, store):
+def pack0(load, store, count=BX):
     lane = lanes(BY)
     first = jnp.zeros((BY, 128), jnp.float32)
     last = jnp.zeros((BY, 128), jnp.float32)
-    for i in range(BX):
+    for i in range(count):
         turned = turn(load(i), 8 * i)
         first = jnp.where((lane >= 8 * i) & (lane < 8 * i + 8), turned, first)
         at = (8 * i - 8) % 128
@@ -208,7 +244,11 @@
 
 def unpack0(land, x, rows):
     dx, i = beside(x, BX)
-    left, right = turn(land[0, dx + 1], -8 * i), turn(land[1, dx + 1], -8 * i)
+    return unpack_columns(land[0, dx + 1], land[1, dx + 1], i, rows)
+
+
+def unpack_columns(left, right, i, rows):
+    left, right = turn(left, -8 * i), turn(right, -8 * i)
     lane = lanes(rows)
     return jnp.where(lane < 8, right, jnp.where(lane >= 120, left, 0.0))
 
@@ -225,13 +265,19 @@
     return out
 
 
-def block_copies(source, land, h, offsets):
+def block_copies(source, land, reach, offsets, edge=None):
     out = []
     for offset in offsets:
         dx, dy, dz = offset
         if dz != 0:
             continue
-        x0, xd, nx = part(dx, BX, h)
+        near, far = edge if edge and dy else reach
+        if dx == 0:
+            x0, xd, nx = 0, 0, BX
+        elif dx > 0:
+            x0, xd, nx = BX - far, -far, far - near + 1
+        else:
+            x0, xd, nx = near - 1, BX + near - 1, far - near + 1
         y0, yd, ny = part(dy, BY, 8)
         out.append((offset, source(x0, nx, y0, ny), land(xd, nx, yd, ny)))
     return out
@@ -257,12 +303,12 @@
 
 def kernel(
     sizes, p_ref, w_ref, out_ref,
-    b0, v0, t0, zs0, zr0, wind, zsw, zrw, velocity, flux,
+    b0, far, sb, v0, t0, zs0, zr0, wind, zsw, zrw, zsx, zrx, coef, velocity, flux,
     vp, zsv, zrv,
     bv, zsb, zrb, s1, l1, zs1, zr1, b1, v1, t1,
     gathered, merged, c2, e2a, e2b,
     rows0, rows2, up1, up0, m_down0, m_down1, m_up1, m_up0,
-    send_sems, recv_sems, load_sems,
+    ruler, send_sems, recv_sems, load_sems,
 ):
     place = Place(sizes)
     load_p = pltpu.make_async_copy(
@@ -275,7 +321,7 @@
     clear_around(b0.at[0], 8, 16, BY)
     for d in range(3):
         clear_around(wind.at[d, 0], 3, 8, BY)
-    clear(zr0, zrw, vp, zrv, bv, zrb, l1, zr1, gathered)
+    clear(far, zr0, zrw, zrx, vp, zrv, bv, zrb, l1, zr1, gathered)
 
     barrier = pltpu.get_barrier_semaphore()
     total = jnp.int32(0)
@@ -303,9 +349,13 @@
     used = [0]
 
     def exchange(copies):
-        base = used[0]
-        used[0] += len(copies)
-        return Exchange(place, ordered(copies), send_sems, recv_sems, base)
+        k = used[0]
+        used[0] += 1
+        return Exchange(place, ordered(copies), send_sems.at[k], recv_sems.at[k], ruler)
+
+    def far_block(x, nx, y, ny):
+        side, lead = (0, 8) if x < 0 else (1, -BX - 5)
+        return far.at[side, pl.ds(x + lead, nx), pl.ds(y + 16, ny), :]
 
     def b0_block(x, nx, y, ny):
         return b0.at[0, pl.ds(x + 8, nx), pl.ds(y + 16, ny), :]
@@ -316,18 +366,35 @@
     def vp_block(x, nx, y, ny):
         return vp.at[pl.ds(x + 2, nx), pl.ds(y + 16, ny), :]
 
+    def wind_side_copies():
+        out = []
+        for offset in AROUND:
+            dx, dy, dz = offset
+            if dx and dz:
+                y0, yd, ny = part(dy, BY, 8)
+                side = 0 if dz > 0 else 1
+                out.append((
+                    offset, zsx.at[side, (dx + 1) // 2, pl.ds(y0, ny), :],
+                    zrx.at[side, (1 - dx) // 2, pl.ds(yd + 8, ny), :]))
+        return out
+
     ex0 = exchange(
-        block_copies(b0_block, b0_block, 8, AROUND)
+        block_copies(b0_block, b0_block, (1, 6), AROUND, (1, 5))
         + rim_copies(
             lambda s, y, ny: zs0.at[s, pl.ds(y, ny), :],
             lambda s, dx, y, ny: zr0.at[s, dx, pl.ds(y + 8, ny), :], AROUND))
+    sides = [d for d in AROUND if d[0]]
+    ex_far = exchange(
+        block_copies(b0_block, far_block, (7, 8), [d for d in sides if d[2] == 0], (6, 7)))
     exw = exchange(
-        block_copies(wind_block, wind_block, 3, AROUND)
+        block_copies(wind_block, wind_block, (1, 3), AROUND, (1, 2))
         + rim_copies(
             lambda s, y, ny: zsw.at[s, :, pl.ds(y, ny), :],
-            lambda s, dx, y, ny: zrw.at[s, dx, :, pl.ds(y + 8, ny), :], AROUND))
+            lambda s, dx, y, ny: zrw.at[s, :, pl.ds(y + 8, ny), :],
+            [d for d in AROUND if not d[0]])
+        + wind_side_copies())
     exv = exchange(
-        block_copies(vp_block, vp_block, 2, NEAR)
+        block_copies(vp_block, vp_block, (1, 2), NEAR, (1, 1))
         + rim_copies(
             lambda s, y, ny: zsv.at[s, pl.ds(y, ny), :],
             lambda s, dx, y, ny: zrv.at[s, dx, pl.ds(y + 8, ny), :], NEAR))
@@ -373,13 +440,16 @@
 
     pl.semaphore_wait(barrier, total)
     ex0.start()
+    ex_far.start()
 
     load_w.wait()
     for d in range(3):
         pack0(lambda i: wind[d, 0, 3 + i, 8:24, :], storer(zsw.at[:, d]))
+    for high, lead in ((0, 3), (1, BX)):
+        pack0(lambda i: wind[i // 3, 0, lead + i % 3, 8:24, :], storer(zsx.at[:, high]), 9)
     exw.start()
 
-    clear(velocity, flux, b1, v1, t1, merged, c2, e2a, e2b, rows2, up1, up0)
+    clear(velocity, flux, sb, b1, v1, t1, merged, c2, e2a, e2b, rows2, up1, up0)
 
     bf16 = jnp.bfloat16
     k = lax.broadcasted_iota(jnp.int32, (128, 128), 0)
@@ -412,8 +482,23 @@
         inside = row_mask(place, first_row, rows, 8)
         return (inside & ((lane < 64) | rim_lanes(place, rows, 64, 72))).astype(jnp.float32)
 
-    def first_two0(reach, r, n, masks):
-        for x in range(-reach, BX + reach):
+    def scaled_masks(masks, factor, weight):
+        factor = factor if weight is None else factor * weight
+        return [m * factor for m in masks]
+
+    def sweep0(target, iterate, x, r, n, masks):
+        weight = slab_weight(place, x, BX)
+        keep, share = scaled_masks(masks, KEEP, weight), scaled_masks(masks, SIXTH, weight)
+        for t, (c, s) in enumerate(six0(iterate, x + 8, r, n)):
+            target[t, x + 8, r : r + n, :] = keep[t] * c + share[t] * s + sb[t, x + 8, r : r + n, :]
+
+    def scale_source(x, r, n, masks):
+        factor = scaled_masks(masks, c0, slab_weight(place, x, BX))
+        for t in range(2):
+            sb[t, x + 8, r : r + n, :] = factor[t] * b0[t, x + 8, r : r + n, :]
+
+    def first_two0(slabs, r, n, masks):
+        for x in slabs:
             weight = slab_weight(place, x, BX)
             for t, (c, s) in enumerate(six0(b0, x + 8, r, n)):
                 value = (1.0 + KEEP) * c0 * c + SIXTH * c0 * s
@@ -496,7 +581,7 @@
     ex0.wait_recv()
     for x in range(-8, BX + 8):
         b0[1, x + 8, 8:40, :] = unpack0(zr0, x, 32)
-    first_two0(7, 8, 32, mask32)
+    first_two0(range(-5, BX + 5), 8, 32, mask32)
     for i in range(10):
         pair = [None, None]
         for x in (2 * i - 4, 2 * i - 3):
@@ -535,10 +620,35 @@
     zsb[1] = low
     exb.start()
     ex0.wait_send()
+    ex_far.wait_recv()
+    for side in range(2):
+        for k in range(3):
+            x = k - 8 if side == 0 else BX + 5 + k
+            distance = -x if side == 0 else x - BX + 1
+            if distance > 6:
+                b0[0, x + 8, 16:32, :] = far[side, k, 16:32, :]
+            if distance < 8:
+                for r in (8, 32):
+                    b0[0, x + 8, r : r + 8, :] = far[side, k, r : r + 8, :]
+    first_two0((-7, -6, -5, BX + 4, BX + 5, BX + 6), 8, 32, mask32)
+    for x in range(-6, BX + 6):
+        scale_source(x, 8, 32, mask32)
+    ex_far.wait_send()
     exw.wait_recv()
-    for d in range(3):
-        for x in range(-3, BX + 3):
-            wind[d, 1, x + 3] = unpack0(zrw.at[:, :, d], x, 32)
+    for x in range(-3, BX + 3):
+        ones = scaled_masks(mask24, 1.0, slab_weight(place, x, BX))
+        halves = scaled_masks(mask24, 0.5, slab_weight(place, x, BX))
+        for d in range(3):
+            if 0 <= x < BX:
+                rim = unpack_columns(zrw[0, d, 4:28, :], zrw[1, d, 4:28, :], x, 24)
+            else:
+                high, i = (0, x + 3) if x < 0 else (1, x - BX)
+                rim = unpack_columns(
+                    zrx[0, high, 4:28, :], zrx[1, high, 4:28, :], 3 * d + i, 24)
+            for t, w in enumerate((wind[d, 0, x + 3, 4:28, :], rim)):
+                half = halves[t] * w
+                coef[d, 0, t, x + 3] = half - ones[t]
+                coef[d, 1, t, x + 3] = -half - ones[t]
     exw.wait_send()
     ex2[0].wait_recv()
     here = coarse(0, 3)
@@ -565,15 +675,9 @@
         for t in range(2):
             v0[t, x + 8, 8:40, :] += scaled(up0[t, (x + 8) // 2], mask32[t], weight)
     for x in range(-6, BX + 6):
-        weight = slab_weight(place, x, BX)
-        for t, (c, s) in enumerate(six0(v0, x + 8, 8, 32)):
-            value = KEEP * c + SIXTH * s + c0 * b0[t, x + 8, 8:40, :]
-            t0[t, x + 8, 8:40, :] = scaled(value, mask32[t], weight)
+        sweep0(t0, v0, x, 8, 32, mask32)
     for x in range(-5, BX + 5):
-        weight = slab_weight(place, x, BX)
-        for t, (c, s) in enumerate(six0(t0, x + 8, 8, 32)):
-            value = KEEP * c + SIXTH * s + c0 * b0[t, x + 8, 8:40, :]
-            v0[t, x + 8, 8:40, :] = scaled(value, mask32[t], weight)
+        sweep0(v0, t0, x, 8, 32, mask32)
     first = v0
 
     for x in range(-4, BX + 4):
@@ -591,7 +695,8 @@
     for x in range(-3, BX + 3):
         weight = slab_weight(place, x, BX)
         i = x + 4
-        half_wind = [[0.5 * wind[e, t, x + 3, 4:28, :] for t in range(2)] for e in range(3)]
+        sevens = scaled_masks(mask24, 7.0, weight)
+        ways = [[[coef[e, k, t, x + 3] for k in range(2)] for e in range(3)] for t in range(2)]
         for d in range(3):
             u = velocity.at[d]
             a, h = u[0, i, 12:36, :], u[1, i, 12:36, :]
@@ -600,14 +705,13 @@
             for t, (c, b, n) in enumerate(((a, ba, na), (h, bh, nh))):
                 x_low, x_high = u[t, i - 1, 12:36, :], u[t, i + 1, 12:36, :]
                 y_low, y_high = u[t, i, 11:35, :], u[t, i, 13:37, :]
-                value = (
-                    7.0 * c
-                    - ((x_low + x_high) + (y_low + y_high) + (b + n))
-                    + half_wind[0][t] * (x_high - x_low)
-                    + half_wind[1][t] * (y_high - y_low)
-                    + half_wind[2][t] * (n - b)
+                along_x, along_y, along_z = ways[t]
+                flux[d, t, x + 3, 4:28, :] = (
+                    sevens[t] * c
+                    + (along_x[0] * x_high + along_x[1] * x_low)
+                    + (along_y[0] * y_high + along_y[1] * y_low)
+                    + (along_z[0] * n + along_z[1] * b)
                 )
-                flux[d, t, x + 3, 4:28, :] = scaled(value, mask24[t], weight)
     for x in range(-2, BX + 2):
         weight = slab_weight(place, x, BX)
         i = x + 3
@@ -622,7 +726,7 @@
             ) * -0.5
             b0[t, x + 8, 12:36, :] = scaled(value, mask24[t], weight)
 
-    first_two0(1, 12, 24, mask24)
+    first_two0(range(-1, BX + 1), 12, 24, mask24)
     for i in range(6):
         pair = None
         for x in (2 * i, 2 * i + 1):
@@ -666,6 +770,8 @@
     ex1.wait_send()
     exv.wait_send()
     exv.wait_recv()
+    for x in range(-1, BX + 1):
+        scale_source(x, 12, 24, mask24)
     for x in range(-2, BX + 2):
         v0[0, x + 8, 12:36, :] = vp[x + 2, 12:36, :]
         v0[1, x + 8, 8:40, :] = unpack0(zrv, x, 32)
@@ -681,19 +787,16 @@
         for t in range(2):
             v0[t, x + 8, 12:36, :] += scaled(up0[t, (x + 2) // 2, 0:24, :], mask24[t], weight)
     for x in range(-1, BX + 1):
-        weight = slab_weight(place, x, BX)
-        for t, (c, s) in enumerate(six0(v0, x + 8, 12, 24)):
-            value = KEEP * c + SIXTH * s + c0 * b0[t, x + 8, 12:36, :]
-            t0[t, x + 8, 12:36, :] = scaled(value, mask24[t], weight)
+        sweep0(t0, v0, x, 12, 24, mask24)
     for x in range(BX):
         ((c, s),) = six0(t0, x + 8, 16, 16, rim=False)
-        out_ref[x] = KEEP * c + SIXTH * s + c0 * b0[0, x + 8, 16:32, :]
+        out_ref[x] = KEEP * c + SIXTH * s + sb[0, x + 8, 16:32, :]
     ex2[1].wait_send()
 
 
 def solution(mesh):
     sizes = tuple(mesh.shape[a] for a in AXES)
-    copies = 26 * 4 + len(NEAR) + len(COARSE[0]) + len(COARSE[1])
+    exchanges = 8
     f32 = jnp.float32
     bf16 = jnp.bfloat16
 
@@ -708,13 +811,18 @@
             out_specs=pl.BlockSpec(memory_space=pltpu.VMEM),
             scratch_shapes=[
                 vmem(2, 28, 48, 128),
+                vmem(2, 3, 48, 128),
+                vmem(2, 28, 48, 128),
                 vmem(2, 28, 48, 128),
                 vmem(2, 28, 48, 128),
                 vmem(2, 16, 128),
                 vmem(2, 3, 32, 128),
-                vmem(3, 2, 18, 32, 128),
+                vmem(3, 1, 18, 32, 128),
                 vmem(2, 3, 16, 128),
-                vmem(2, 3, 3, 32, 128),
+                vmem(2, 3, 32, 128),
+                vmem(2, 2, 16, 128),
+                vmem(2, 2, 32, 128),
+                vmem(3, 2, 2, 18, 24, 128),
                 vmem(3, 2, 20, 48, 128),
                 vmem(3, 2, 18, 32, 128),
                 vmem(16, 48, 128),
@@ -743,8 +851,9 @@
                 vmem(384, 128, dtype=bf16),
                 vmem(128, 128, dtype=bf16),
                 vmem(128, 256, dtype=bf16),
-                pltpu.SemaphoreType.DMA((copies,)),
-                pltpu.SemaphoreType.DMA((copies,)),
+                vmem(512, 4, 128),
+                pltpu.SemaphoreType.DMA((exchanges,)),
+                pltpu.SemaphoreType.DMA((exchanges,)),
                 pltpu.SemaphoreType.DMA((2,)),
             ],
             compiler_params=pltpu.CompilerParams(

time: 49.6 us -> 43.1 us (0.87)
  Pallas kernels: 47.9 us -> 41.5 us
    pallas_call x1, Pallas kernels: 47.9 us -> 41.5 us  [body(): pl.pallas_call(functools.partial(kernel, sizes), out_shape=jax.ShapeDtype...]
where the time goes in v3:
time: 43.1 us; the launch traced here: 43 us
  Pallas kernels  41.5 us (96%)
  local copies, waits for them, and re-layouts  1.54 us (4%)
    pallas_call x1, Pallas kernels, body(): pl.pallas_call(functools.partial(kernel, sizes), out_shape=jax.ShapeDtype...  41.5 us
    unnamed x1, local copies, waits for them, and re-layouts  1.54 us

profile of v3, /device:TPU:1, one launch (start us, length us, event | category | flops | bytes accessed | tf_op | source)
XLA Modules:
  0.0 43.0 jit_solution(7561152554198396254)
XLA Ops:
  0.0 41.5 %schur.1 = f32[12,16,128]{2,1,0:T(8,128)} custom-call(f32[12,16,128]{2,1,0:T(8,128)} %p_ref.1, f32[3,12,16,128]{3,2,1,0:T(8,128)} %w_ref.1), custom_call_target="tpu_custom_call" | custom-call | tf_op jit(solution)/shard_map/schur/pallas_call | solution.py:807
  41.5 1.5 %copy.4 = f32[12,16,128]{2,1,0:T(8,128)} copy(f32[12,16,128]{2,1,0:T(8,128)} %schur.1) | data formatting | bytes 196608

commit v4 on v3

--- a/solution.py
+++ b/solution.py
@@ -42,7 +42,7 @@
 
 
 COARSE = (coarse_offsets(True), coarse_offsets(False))
-GREETED = coarse_offsets(True)
+GREETED = AROUND
 
 
 def part(delta, count, width):

time: 43.1 us -> 42.8 us (level)
  no operation moved by 1% of the time
where the time goes in v4:
time: 42.8 us; the launch traced here: 42.6 us
  Pallas kernels  41.1 us (96%)
  local copies, waits for them, and re-layouts  1.54 us (4%)
    pallas_call x1, Pallas kernels, body(): pl.pallas_call(functools.partial(kernel, sizes), out_shape=jax.ShapeDtype...  41.1 us
    unnamed x1, local copies, waits for them, and re-layouts  1.54 us

profile of v4, /device:TPU:1, one launch (start us, length us, event | category | flops | bytes accessed | tf_op | source)
XLA Modules:
  0.0 42.6 jit_solution(7070120822533005054)
XLA Ops:
  0.0 41.1 %schur.1 = f32[12,16,128]{2,1,0:T(8,128)} custom-call(f32[12,16,128]{2,1,0:T(8,128)} %p_ref.1, f32[3,12,16,128]{3,2,1,0:T(8,128)} %w_ref.1), custom_call_target="tpu_custom_call" | custom-call | tf_op jit(solution)/shard_map/schur/pallas_call | solution.py:807
  41.1 1.5 %copy.4 = f32[12,16,128]{2,1,0:T(8,128)} copy(f32[12,16,128]{2,1,0:T(8,128)} %schur.1) | data formatting | bytes 196608

commit v5 on v4

--- a/solution.py
+++ b/solution.py
@@ -305,7 +305,7 @@
     sizes, p_ref, w_ref, out_ref,
     b0, far, sb, v0, t0, zs0, zr0, wind, zsw, zrw, zsx, zrx, coef, velocity, flux,
     vp, zsv, zrv,
-    bv, zsb, zrb, s1, l1, zs1, zr1, b1, v1, t1,
+    bv, zsb, zrb, s1, l1, l1_far, zs1, zr1, zr1_far, b1, v1, t1,
     gathered, merged, c2, e2a, e2b,
     rows0, rows2, up1, up0, m_down0, m_down1, m_up1, m_up0,
     ruler, send_sems, recv_sems, load_sems,
@@ -321,7 +321,7 @@
     clear_around(b0.at[0], 8, 16, BY)
     for d in range(3):
         clear_around(wind.at[d, 0], 3, 8, BY)
-    clear(far, zr0, zrw, zrx, vp, zrv, bv, zrb, l1, zr1, gathered)
+    clear(far, zr0, zrw, zrx, vp, zrv, bv, zrb, l1, l1_far, zr1, zr1_far, gathered)
 
     barrier = pltpu.get_barrier_semaphore()
     total = jnp.int32(0)
@@ -413,19 +413,25 @@
                     offset, zsb.at[side], zrb.at[side, 1 - dx, pl.ds(8 - 8 * dy, 8), :]))
         return out
 
-    def level1_copies():
+    def level1_copies(reach, edge, offsets, blocks, rims):
         out = []
-        for offset in AROUND:
+        for offset in offsets:
             dx, dy, dz = offset
             if dz == 0:
-                x0, xd, nx = part(dx, 6, 4)
+                near, far_end = edge if dx and dy else reach
+                if dx == 0:
+                    x0, xd, nx = 0, 0, 6
+                elif dx > 0:
+                    x0, xd, nx = 6 - far_end, -far_end, far_end - near + 1
+                else:
+                    x0, xd, nx = near - 1, 5 + near, far_end - near + 1
                 out.append((
                     offset, s1.at[pl.ds(x0, nx)],
-                    l1.at[pl.ds(xd + 4, nx), pl.ds(8 - 8 * dy, 8), :]))
+                    blocks.at[pl.ds(xd + 4, nx), pl.ds(8 - 8 * dy, 8), :]))
             else:
                 side = 0 if dz > 0 else 1
                 out.append((
-                    offset, zs1.at[side], zr1.at[side, 1 - dx, pl.ds(8 - 8 * dy, 8), :]))
+                    offset, zs1.at[side], rims.at[side, 1 - dx, pl.ds(8 - 8 * dy, 8), :]))
         return out
 
     def coarse_copies(number):
@@ -435,7 +441,9 @@
         ]
 
     exb = exchange(bv_copies())
-    ex1 = exchange(level1_copies())
+    ex1 = exchange(level1_copies((1, 2), (1, 1), NEAR, l1, zr1))
+    ex1_far = exchange(level1_copies(
+        (3, 4), (2, 3), [d for d in AROUND if d[0] and (d[2] == 0 or d[1])], l1_far, zr1_far))
     ex2 = [exchange(coarse_copies(0)), exchange(coarse_copies(1))]
 
     pl.semaphore_wait(barrier, total)
@@ -499,10 +507,9 @@
 
     def first_two0(slabs, r, n, masks):
         for x in slabs:
-            weight = slab_weight(place, x, BX)
+            factors = scaled_masks(masks, c0, slab_weight(place, x, BX))
             for t, (c, s) in enumerate(six0(b0, x + 8, r, n)):
-                value = (1.0 + KEEP) * c0 * c + SIXTH * c0 * s
-                v0[t, x + 8, r : r + n, :] = scaled(value, masks[t], weight)
+                v0[t, x + 8, r : r + n, :] = factors[t] * ((1.0 + KEEP) * c + SIXTH * s)
 
     def down1_and_send(number, r, n):
         pairs = []
@@ -665,19 +672,20 @@
                 jnp.where(lane24 < 72, turn(right, 64 - 8 * i - lead),
                           jnp.where(lane24 >= 120, turn(left, 120 - 8 * i - lead), 0.0)))
             if ref is v1:
-                value = value + scaled(
-                    up1[(x + 6) // 2, 0:24, :], mask, slab_weight(place, x, 6))
+                value = value + up1[(x + 6) // 2, 0:24, :]
             ref[x + 6, 8:32, :] = value
     last_two1(4, 8, 24, mask)
     spread0(4, 16)
     for x in range(-7, BX + 7):
-        weight = slab_weight(place, x, BX)
         for t in range(2):
-            v0[t, x + 8, 8:40, :] += scaled(up0[t, (x + 8) // 2], mask32[t], weight)
-    for x in range(-6, BX + 6):
-        sweep0(t0, v0, x, 8, 32, mask32)
-    for x in range(-5, BX + 5):
-        sweep0(v0, t0, x, 8, 32, mask32)
+            v0[t, x + 8, 8:40, :] += up0[t, (x + 8) // 2]
+    for reach, target, iterate in ((6, t0, v0), (5, v0, t0)):
+        for x in range(-reach, BX + reach):
+            away = max(-x, x - BX + 1, 0)
+            if reach - away <= 4:
+                sweep0(target, iterate, x, 12, 24, mask24)
+            else:
+                sweep0(target, iterate, x, 8, 32, mask32)
     first = v0
 
     for x in range(-4, BX + 4):
@@ -713,7 +721,7 @@
                     + (along_z[0] * n + along_z[1] * b)
                 )
     for x in range(-2, BX + 2):
-        weight = slab_weight(place, x, BX)
+        halves = scaled_masks(mask24, -0.5, slab_weight(place, x, BX))
         i = x + 3
         a, h = flux[2, 0, i, 4:28, :], flux[2, 1, i, 4:28, :]
         ba, bh = z_back(a, h)
@@ -723,8 +731,8 @@
                 (flux[0, t, i + 1, 4:28, :] - flux[0, t, i - 1, 4:28, :])
                 + (flux[1, t, i, 5:29, :] - flux[1, t, i, 3:27, :])
                 + (n - b)
-            ) * -0.5
-            b0[t, x + 8, 12:36, :] = scaled(value, mask24[t], weight)
+            )
+            b0[t, x + 8, 12:36, :] = value * halves[t]
 
     first_two0(range(-1, BX + 1), 12, 24, mask24)
     for i in range(6):
@@ -748,6 +756,7 @@
     zs1[0] = high
     zs1[1] = low
     ex1.start()
+    ex1_far.start()
     for x in range(BX):
         vp[x + 2, 16:32, :] = v0[0, x + 8, 16:32, :]
     pack0(lambda i: v0[0, 8 + i, 16:32, :], storer(zsv))
@@ -755,19 +764,32 @@
     ex2[0].wait_send()
     exb.wait_send()
     ex1.wait_recv()
-    for x in range(-4, 10):
-        dx, i = beside(x, 6)
-        b1[x + 6, 8:32, :] = jnp.where(
-            lane24 < 64, l1[x + 4],
-            jnp.where(lane24 < 72, turn(zr1[1, dx + 1], 64 - 8 * i),
-                      jnp.where(lane24 >= 120, turn(zr1[0, dx + 1], 120 - 8 * i), 0.0)))
     mask = level1_mask(-4, 16)
-    for x in range(-3, 9):
-        c, s = six1(b1, x + 6, 12, 16)
-        value = (1.0 + KEEP) * c1 * c + SIXTH * c1 * s
-        v1[x + 6, 12:28, :] = scaled(value, mask, slab_weight(place, x, 6))
+
+    def source1(slabs, block, rim):
+        for x in slabs:
+            dx, i = beside(x, 6)
+            b1[x + 6, 8:32, :] = jnp.where(
+                lane24 < 64, block(x + 4),
+                jnp.where(lane24 < 72, turn(rim(1, dx + 1), 64 - 8 * i),
+                          jnp.where(lane24 >= 120, turn(rim(0, dx + 1), 120 - 8 * i), 0.0)))
+
+    def first_two1(reach):
+        for x in range(-reach, 6 + reach):
+            factors = scaled_masks((mask,), c1, slab_weight(place, x, 6))
+            c, s = six1(b1, x + 6, 12, 16)
+            v1[x + 6, 12:28, :] = factors[0] * ((1.0 + KEEP) * c + SIXTH * s)
+
+    source1(range(-2, 8), lambda k: l1[k], lambda side, k: zr1[side, k])
+    first_two1(1)
     down1_and_send(1, 12, 16)
+    ex1_far.wait_recv()
+    source1(
+        range(-4, 10), lambda k: l1[k] + l1_far[k],
+        lambda side, k: zr1[side, k] + zr1_far[side, k])
+    first_two1(3)
     ex1.wait_send()
+    ex1_far.wait_send()
     exv.wait_send()
     exv.wait_recv()
     for x in range(-1, BX + 1):
@@ -779,13 +801,12 @@
     here = coarse(1, 2)
     spread1(here, 2, -2, 8)
     for x in range(-3, 9):
-        v1[x + 6, 12:28, :] += scaled(up1[(x + 4) // 2, 0:16, :], mask, slab_weight(place, x, 6))
+        v1[x + 6, 12:28, :] += up1[(x + 4) // 2, 0:16, :]
     last_two1(1, 12, 16, mask)
     spread0(1, 12)
     for x in range(-2, BX + 2):
-        weight = slab_weight(place, x, BX)
         for t in range(2):
-            v0[t, x + 8, 12:36, :] += scaled(up0[t, (x + 2) // 2, 0:24, :], mask24[t], weight)
+            v0[t, x + 8, 12:36, :] += up0[t, (x + 2) // 2, 0:24, :]
     for x in range(-1, BX + 1):
         sweep0(t0, v0, x, 12, 24, mask24)
     for x in range(BX):
@@ -796,7 +817,7 @@
 
 def solution(mesh):
     sizes = tuple(mesh.shape[a] for a in AXES)
-    exchanges = 8
+    exchanges = 9
     f32 = jnp.float32
     bf16 = jnp.bfloat16
 
@@ -833,7 +854,9 @@
                 vmem(2, 3, 24, 128),
                 vmem(6, 8, 128),
                 vmem(14, 24, 128),
+                vmem(14, 24, 128),
                 vmem(2, 8, 128),
+                vmem(2, 3, 24, 128),
                 vmem(2, 3, 24, 128),
                 vmem(18, 40, 128),
                 vmem(18, 40, 128),
@@ -857,7 +880,7 @@
                 pltpu.SemaphoreType.DMA((2,)),
             ],
             compiler_params=pltpu.CompilerParams(
-                collective_id=0, has_side_effects=True, vmem_limit_bytes=67043328
+                collective_id=0, has_side_effects=True, vmem_limit_bytes=56400000
             ),
             name="schur",
         )(pressure, wind)

time: 42.8 us -> 40.6 us (0.949)
  Pallas kernels: 41.1 us -> 39.8 us
  local copies, waits for them, and re-layouts: 1.54 us -> 0.64 us
    pallas_call x1, Pallas kernels: 41.1 us -> 39.8 us  [body(): pl.pallas_call(functools.partial(kernel, sizes), out_shape=jax.ShapeDtype...]
    unnamed x1, local copies, waits for them, and re-layouts: 1.54 us -> 0.64 us
where the time goes in v5:
time: 40.6 us; the launch traced here: 40.5 us
  Pallas kernels  39.8 us (98%)
  local copies, waits for them, and re-layouts  0.64 us (2%)
    pallas_call x1, Pallas kernels, body(): pl.pallas_call(functools.partial(kernel, sizes), out_shape=jax.ShapeDtype...  39.8 us

profile of v5, /device:TPU:1, one launch (start us, length us, event | category | flops | bytes accessed | tf_op | source)
XLA Modules:
  0.0 40.5 jit_solution(16310137911994993497)
XLA Ops:
  0.0 39.8 %schur.1 = f32[12,16,128]{2,1,0:T(8,128)S(1)} custom-call(f32[12,16,128]{2,1,0:T(8,128)} %p_ref.1, f32[3,12,16,128]{3,2,1,0:T(8,128)} %w_ref.1), custom_call_target="tpu_custom_call" | custom-call | tf_op jit(solution)/shard_map/schur/pallas_call | solution.py:828
  39.9 0.6 %copy.4 = f32[12,16,128]{2,1,0:T(8,128)} copy(f32[12,16,128]{2,1,0:T(8,128)S(1)} %schur.1) | data formatting | bytes 196608

commit v6 on v5

--- a/solution.py
+++ b/solution.py
@@ -143,8 +143,9 @@
 
 def row_mask(place, first_row, rows, extent):
     y = first_row + lax.broadcasted_iota(jnp.int32, (rows, 128), 0)
-    low = jnp.where(place.has[1][-1], -64, 0)
-    high = jnp.where(place.has[1][1], 64, extent)
+    has = place.has[1]
+    low = jnp.where(has[-2], -64, jnp.where(has[-1], -extent, 0))
+    high = jnp.where(has[2], 64, jnp.where(has[1], 2 * extent, extent))
     return (y >= low) & (y < high)
 
 
@@ -156,11 +157,9 @@
 
 
 def slab_weight(place, x, extent):
-    if x < 0:
-        return place.has[0][-1].astype(jnp.float32)
-    if x >= extent:
-        return place.has[0][1].astype(jnp.float32)
-    return None
+    if 0 <= x < extent:
+        return None
+    return place.has[0][x // extent].astype(jnp.float32)
 
 
 def z_back(a, h):
@@ -443,7 +442,7 @@
     exb = exchange(bv_copies())
     ex1 = exchange(level1_copies((1, 2), (1, 1), NEAR, l1, zr1))
     ex1_far = exchange(level1_copies(
-        (3, 4), (2, 3), [d for d in AROUND if d[0] and (d[2] == 0 or d[1])], l1_far, zr1_far))
+        (3, 4), (2, 4), [d for d in AROUND if d[0] and (d[2] == 0 or d[1])], l1_far, zr1_far))
     ex2 = [exchange(coarse_copies(0)), exchange(coarse_copies(1))]
 
     pl.semaphore_wait(barrier, total)

time: 40.6 us -> 40.8 us (level)
  no operation moved by 1% of the time
where the time goes in v6:
time: 40.8 us; the launch traced here: 40.7 us
  Pallas kernels  40 us (98%)
  local copies, waits for them, and re-layouts  0.64 us (2%)
    pallas_call x1, Pallas kernels, body(): pl.pallas_call(functools.partial(kernel, sizes), out_shape=jax.ShapeDtype...  40 us

profile of v6, /device:TPU:1, one launch (start us, length us, event | category | flops | bytes accessed | tf_op | source)
XLA Modules:
  0.0 40.7 jit_solution(9087240804531083076)
XLA Ops:
  0.0 40.0 %schur.1 = f32[12,16,128]{2,1,0:T(8,128)S(1)} custom-call(f32[12,16,128]{2,1,0:T(8,128)} %p_ref.1, f32[3,12,16,128]{3,2,1,0:T(8,128)} %w_ref.1), custom_call_target="tpu_custom_call" | custom-call | tf_op jit(solution)/shard_map/schur/pallas_call | solution.py:827
  40.0 0.6 %copy.4 = f32[12,16,128]{2,1,0:T(8,128)} copy(f32[12,16,128]{2,1,0:T(8,128)S(1)} %schur.1) | data formatting | bytes 196608

commit v7 on v6

--- a/solution.py
+++ b/solution.py
@@ -320,7 +320,7 @@
     clear_around(b0.at[0], 8, 16, BY)
     for d in range(3):
         clear_around(wind.at[d, 0], 3, 8, BY)
-    clear(far, zr0, zrw, zrx, vp, zrv, bv, zrb, l1, l1_far, zr1, zr1_far, gathered)
+    clear(far, zr0, zrw, zrx, gathered)
 
     barrier = pltpu.get_barrier_semaphore()
     total = jnp.int32(0)
@@ -341,6 +341,7 @@
             ref[1] = f
         return store
 
+    clear(vp, zrv, bv, zrb, l1, l1_far, zr1, zr1_far)
     clear(b0.at[1], v0, t0, rows0)
     load_p.wait()
     pack0(lambda i: b0[0, 8 + i, 16:32, :], storer(zs0))
@@ -483,6 +484,16 @@
     m32a, m32h = masks0(place, -8, 32)
     m24a, m24h = masks0(place, -4, 24)
     mask32, mask24 = (m32a, m32h), (m24a, m24h)
+    mask16 = masks0(place, 0, 16)
+
+    def span(reach, x):
+        left = reach - max(-x, x - BX + 1, 0)
+        if left <= 0:
+            return 16, 16, mask16, False
+        if left <= 4:
+            return 12, 24, mask24, True
+        return 8, 32, mask32, True
+
 
     def level1_mask(first_row, rows):
         lane = lanes(rows)
@@ -493,10 +504,11 @@
         factor = factor if weight is None else factor * weight
         return [m * factor for m in masks]
 
-    def sweep0(target, iterate, x, r, n, masks):
+    def sweep0(target, iterate, x, reach):
+        r, n, masks, rim = span(reach, x)
         weight = slab_weight(place, x, BX)
         keep, share = scaled_masks(masks, KEEP, weight), scaled_masks(masks, SIXTH, weight)
-        for t, (c, s) in enumerate(six0(iterate, x + 8, r, n)):
+        for t, (c, s) in enumerate(six0(iterate, x + 8, r, n, rim)):
             target[t, x + 8, r : r + n, :] = keep[t] * c + share[t] * s + sb[t, x + 8, r : r + n, :]
 
     def scale_source(x, r, n, masks):
@@ -504,10 +516,11 @@
         for t in range(2):
             sb[t, x + 8, r : r + n, :] = factor[t] * b0[t, x + 8, r : r + n, :]
 
-    def first_two0(slabs, r, n, masks):
+    def first_two0(slabs, reach):
         for x in slabs:
+            r, n, masks, rim = span(reach, x)
             factors = scaled_masks(masks, c0, slab_weight(place, x, BX))
-            for t, (c, s) in enumerate(six0(b0, x + 8, r, n)):
+            for t, (c, s) in enumerate(six0(b0, x + 8, r, n, rim)):
                 v0[t, x + 8, r : r + n, :] = factors[t] * ((1.0 + KEEP) * c + SIXTH * s)
 
     def down1_and_send(number, r, n):
@@ -585,17 +598,19 @@
                 up0[t, j, pl.ds(1, n, stride=2), :] = value
 
     ex0.wait_recv()
-    for x in range(-8, BX + 8):
-        b0[1, x + 8, 8:40, :] = unpack0(zr0, x, 32)
-    first_two0(range(-5, BX + 5), 8, 32, mask32)
+    for x in range(-6, BX + 6):
+        r, n = span(6, x)[:2]
+        b0[1, x + 8, r : r + n, :] = unpack0(zr0.at[:, :, pl.ds(r - 8, n), :], x, n)
+    first_two0(range(-5, BX + 5), 5)
     for i in range(10):
         pair = [None, None]
+        r, n, rim = (12, 24, True) if 0 < i < 9 else (16, 16, False)
         for x in (2 * i - 4, 2 * i - 3):
-            for t, (c, s) in enumerate(six0(v0, x + 8, 12, 24)):
-                res = b0[t, x + 8, 12:36, :] - (6.0 * c - s)
+            for t, (c, s) in enumerate(six0(v0, x + 8, r, n, rim)):
+                res = b0[t, x + 8, r : r + n, :] - (6.0 * c - s)
                 pair[t] = res if pair[t] is None else pair[t] + res
-        for t in range(2):
-            rows0[t, i, 0:24, :] = pair[t]
+        for t in range(1 + rim):
+            rows0[t, i, r - 12 : r - 12 + n, :] = pair[t]
     cells = [
         jnp.concatenate(
             [rows0[t, i, pl.ds(0, 16, stride=2), :] + rows0[t, i, pl.ds(1, 16, stride=2), :]
@@ -636,7 +651,10 @@
             if distance < 8:
                 for r in (8, 32):
                     b0[0, x + 8, r : r + 8, :] = far[side, k, r : r + 8, :]
-    first_two0((-7, -6, -5, BX + 4, BX + 5, BX + 6), 8, 32, mask32)
+    outer = [x for k in range(1, 9) for x in (-k, BX - 1 + k)]
+    for x in outer:
+        b0[1, x + 8, 8:40, :] = unpack0(zr0, x, 32)
+    first_two0(outer[:14], 7)
     for x in range(-6, BX + 6):
         scale_source(x, 8, 32, mask32)
     ex_far.wait_send()
@@ -680,60 +698,65 @@
             v0[t, x + 8, 8:40, :] += up0[t, (x + 8) // 2]
     for reach, target, iterate in ((6, t0, v0), (5, v0, t0)):
         for x in range(-reach, BX + reach):
-            away = max(-x, x - BX + 1, 0)
-            if reach - away <= 4:
-                sweep0(target, iterate, x, 12, 24, mask24)
-            else:
-                sweep0(target, iterate, x, 8, 32, mask32)
+            sweep0(target, iterate, x, reach)
     first = v0
 
     for x in range(-4, BX + 4):
-        weight = slab_weight(place, x, BX)
-        half = 0.5 if weight is None else 0.5 * weight
+        r, n, masks, rim = span(4, x)
+        halves = scaled_masks(masks, 0.5, slab_weight(place, x, BX))
         i = x + 8
-        a, h = first[0, i, 12:36, :], first[1, i, 12:36, :]
+        rows = slice(r, r + n)
+        a, h = first[0, i, rows, :], first[1, i, rows, :]
         ba, bh = z_back(a, h)
         na, nh = z_next(a, h)
-        for t, (b, n) in enumerate(((ba, na), (bh, nh))):
-            m = mask24[t] * half
-            velocity[0, t, x + 4, 12:36, :] = (first[t, i + 1, 12:36, :] - first[t, i - 1, 12:36, :]) * m
-            velocity[1, t, x + 4, 12:36, :] = (first[t, i, 13:37, :] - first[t, i, 11:35, :]) * m
-            velocity[2, t, x + 4, 12:36, :] = (n - b) * m
+        for t, (back, ahead) in enumerate(((ba, na), (bh, nh))[: 1 + rim]):
+            m = halves[t]
+            velocity[0, t, x + 4, rows, :] = (first[t, i + 1, rows, :] - first[t, i - 1, rows, :]) * m
+            velocity[1, t, x + 4, rows, :] = (
+                first[t, i, r + 1 : r + 1 + n, :] - first[t, i, r - 1 : r - 1 + n, :]) * m
+            velocity[2, t, x + 4, rows, :] = (ahead - back) * m
     for x in range(-3, BX + 3):
-        weight = slab_weight(place, x, BX)
+        r, n, masks, rim = span(3, x)
         i = x + 4
-        sevens = scaled_masks(mask24, 7.0, weight)
-        ways = [[[coef[e, k, t, x + 3] for k in range(2)] for e in range(3)] for t in range(2)]
+        rows, low_rows = slice(r, r + n), slice(r - 8, r - 8 + n)
+        sevens = scaled_masks(masks, 7.0, slab_weight(place, x, BX))
+        ways = [
+            [[coef[e, k, t, x + 3, r - 12 : r - 12 + n, :] for k in range(2)] for e in range(3)]
+            for t in range(1 + rim)
+        ]
         for d in range(3):
             u = velocity.at[d]
-            a, h = u[0, i, 12:36, :], u[1, i, 12:36, :]
+            a, h = u[0, i, rows, :], u[1, i, rows, :]
             ba, bh = z_back(a, h)
             na, nh = z_next(a, h)
-            for t, (c, b, n) in enumerate(((a, ba, na), (h, bh, nh))):
-                x_low, x_high = u[t, i - 1, 12:36, :], u[t, i + 1, 12:36, :]
-                y_low, y_high = u[t, i, 11:35, :], u[t, i, 13:37, :]
+            for t, (c, back, ahead) in enumerate(((a, ba, na), (h, bh, nh))[: 1 + rim]):
+                x_low, x_high = u[t, i - 1, rows, :], u[t, i + 1, rows, :]
+                y_low, y_high = u[t, i, r - 1 : r - 1 + n, :], u[t, i, r + 1 : r + 1 + n, :]
                 along_x, along_y, along_z = ways[t]
-                flux[d, t, x + 3, 4:28, :] = (
+                flux[d, t, x + 3, low_rows, :] = (
                     sevens[t] * c
                     + (along_x[0] * x_high + along_x[1] * x_low)
                     + (along_y[0] * y_high + along_y[1] * y_low)
-                    + (along_z[0] * n + along_z[1] * b)
+                    + (along_z[0] * ahead + along_z[1] * back)
                 )
     for x in range(-2, BX + 2):
-        halves = scaled_masks(mask24, -0.5, slab_weight(place, x, BX))
+        r, n, masks, rim = span(2, x)
+        halves = scaled_masks(masks, -0.5, slab_weight(place, x, BX))
         i = x + 3
-        a, h = flux[2, 0, i, 4:28, :], flux[2, 1, i, 4:28, :]
+        q = r - 8
+        rows = slice(q, q + n)
+        a, h = flux[2, 0, i, rows, :], flux[2, 1, i, rows, :]
         ba, bh = z_back(a, h)
         na, nh = z_next(a, h)
-        for t, (b, n) in enumerate(((ba, na), (bh, nh))):
+        for t, (back, ahead) in enumerate(((ba, na), (bh, nh))[: 1 + rim]):
             value = (
-                (flux[0, t, i + 1, 4:28, :] - flux[0, t, i - 1, 4:28, :])
-                + (flux[1, t, i, 5:29, :] - flux[1, t, i, 3:27, :])
-                + (n - b)
+                (flux[0, t, i + 1, rows, :] - flux[0, t, i - 1, rows, :])
+                + (flux[1, t, i, q + 1 : q + 1 + n, :] - flux[1, t, i, q - 1 : q - 1 + n, :])
+                + (ahead - back)
             )
-            b0[t, x + 8, 12:36, :] = value * halves[t]
-
-    first_two0(range(-1, BX + 1), 12, 24, mask24)
+            b0[t, x + 8, r : r + n, :] = value * halves[t]
+
+    first_two0(range(-1, BX + 1), 1)
     for i in range(6):
         pair = None
         for x in (2 * i, 2 * i + 1):
@@ -807,7 +830,7 @@
         for t in range(2):
             v0[t, x + 8, 12:36, :] += up0[t, (x + 2) // 2, 0:24, :]
     for x in range(-1, BX + 1):
-        sweep0(t0, v0, x, 12, 24, mask24)
+        sweep0(t0, v0, x, 1)
     for x in range(BX):
         ((c, s),) = six0(t0, x + 8, 16, 16, rim=False)
         out_ref[x] = KEEP * c + SIXTH * s + sb[0, x + 8, 16:32, :]

time: 40.8 us -> 40.6 us (level)
  no operation moved by 1% of the time
where the time goes in v7:
time: 40.6 us; the launch traced here: 40.4 us
  Pallas kernels  39.8 us (98%)
  local copies, waits for them, and re-layouts  0.64 us (2%)
    pallas_call x1, Pallas kernels, body(): pl.pallas_call(functools.partial(kernel, sizes), out_shape=jax.ShapeDtype...  39.8 us

profile of v7, /device:TPU:1, one launch (start us, length us, event | category | flops | bytes accessed | tf_op | source)
XLA Modules:
  0.0 40.4 jit_solution(397054481297707448)
XLA Ops:
  0.0 39.8 %schur.1 = f32[12,16,128]{2,1,0:T(8,128)S(1)} custom-call(f32[12,16,128]{2,1,0:T(8,128)} %p_ref.1, f32[3,12,16,128]{3,2,1,0:T(8,128)} %w_ref.1), custom_call_target="tpu_custom_call" | custom-call | tf_op jit(solution)/shard_map/schur/pallas_call | solution.py:850
  39.8 0.6 %copy.4 = f32[12,16,128]{2,1,0:T(8,128)} copy(f32[12,16,128]{2,1,0:T(8,128)S(1)} %schur.1) | data formatting | bytes 196608

commit v8 on v7

--- a/solution.py
+++ b/solution.py
@@ -404,9 +404,11 @@
         for offset in AROUND:
             dx, dy, dz = offset
             if dz == 0:
+                n = 5 if dx and dy else 6
+                skip = 6 - n if dx > 0 else 0
                 out.append((
-                    offset, bv.at[pl.ds(6, 6), pl.ds(16, 8), :],
-                    bv.at[pl.ds(6 - 6 * dx, 6), pl.ds(16 - 8 * dy, 8), :]))
+                    offset, bv.at[pl.ds(6 + skip, n), pl.ds(16, 8), :],
+                    bv.at[pl.ds(6 - 6 * dx + skip, n), pl.ds(16 - 8 * dy, 8), :]))
             else:
                 side = 0 if dz > 0 else 1
                 out.append((

time: 40.6 us -> 40.5 us (level)
  no operation moved by 1% of the time
where the time goes in v8:
time: 40.5 us; the launch traced here: 40.3 us
  Pallas kernels  39.7 us (98%)
  local copies, waits for them, and re-layouts  0.64 us (2%)
    pallas_call x1, Pallas kernels, body(): pl.pallas_call(functools.partial(kernel, sizes), out_shape=jax.ShapeDtype...  39.7 us

profile of v8, /device:TPU:1, one launch (start us, length us, event | category | flops | bytes accessed | tf_op | source)
XLA Modules:
  0.0 40.3 jit_solution(11205991609888203015)
XLA Ops:
  0.0 39.7 %schur.1 = f32[12,16,128]{2,1,0:T(8,128)S(1)} custom-call(f32[12,16,128]{2,1,0:T(8,128)} %p_ref.1, f32[3,12,16,128]{3,2,1,0:T(8,128)} %w_ref.1), custom_call_target="tpu_custom_call" | custom-call | tf_op jit(solution)/shard_map/schur/pallas_call | solution.py:852
  39.7 0.6 %copy.4 = f32[12,16,128]{2,1,0:T(8,128)} copy(f32[12,16,128]{2,1,0:T(8,128)S(1)} %schur.1) | data formatting | bytes 196608
